TPU v7x, 32 devices: a 4x4x1 block of a 4x4x8 slice. The times are simulated.
32 devices in a mesh: batch: 1 (over z), col: 4 (over y), row: 8 (over x, core).
Axes of the slice: x: 4, y: 4, z: 1, core: 2. Of those that a mesh axis runs over, the one named last changes fastest.
The devices are a block of a 4x4x8 slice.
Arguments:
- field: float32 [2048, 1024, 16], P(('batch', 'row'), 'col')
- lower_x: float32 [2048, 1024], P(('batch', 'row'), 'col')
- diag_x: float32 [2048, 1024], P(('batch', 'row'), 'col')
- upper_x: float32 [2048, 1024], P(('batch', 'row'), 'col')
- lower_y: float32 [2048, 1024], P(('batch', 'row'), 'col')
- diag_y: float32 [2048, 1024], P(('batch', 'row'), 'col')
- upper_y: float32 [2048, 1024], P(('batch', 'row'), 'col')
Outputs:
- output: float32 [2048, 1024, 16], P(('batch', 'row'), 'col')
All inputs are finite; a program needn't handle non-finite values.
Results may differ from a plain program's by a relative error of at most 0.001.
Values sent between devices are 32-bit elements.
A program may use at most 768 MiB of HBM per device.

v0:
```python
import functools

import jax
import jax.numpy as jnp
from jax import lax
from jax.experimental import pallas as pl
from jax.experimental.pallas import tpu as pltpu
from jax.sharding import PartitionSpec as P

STEPS = 3
F32 = jnp.float32
LANES = 128
SUB = 8
MESH = pl.DeviceIdType.MESH
X, Y = 0, 1


def adi_kernel(axes, field, lower_x, diag_x, upper_x, lower_y, diag_y, upper_y, out,
               nat, rx, ry, hs, pa, pb, pc, nd, md, ne, me_, ln, cn, un, an, m2, d2, w2, v2, r0, rn,
               gs, gc_x, gc_y, red_x, red_y, sx, sy, ex, ey, gt, ss, halo_s, halo_r,
               in_sem, out_sem, gsend_x, gsend_y, grecv_x, grecv_y, ssx, ssy, rsx, rsy, hsend, hrecv):
    (row_name, parts_x), (col_name, parts_y) = axes
    n = lower_x.shape[0]
    tiles = n // LANES
    chunks = field.shape[1] // SUB
    pitch = 2 * tiles
    half = n // 2
    pos = (lax.axis_index(row_name), lax.axis_index(col_name))
    parts = (parts_x, parts_y)
    names = (row_name, col_name)
    exch = (ex, ey)
    send = (sx, sy)
    send_sems = (ssx, ssy)
    recv_sems = (rsx, rsy)
    gather = (gc_x, gc_y)
    reduced = (red_x, red_y)

    def others(axis):
        return [lax.rem(pos[axis] + off, parts[axis]) for off in range(1, parts[axis])]

    loads = []
    for slot, ref in enumerate((lower_x, diag_x, upper_x, lower_y, diag_y, upper_y)):
        loads.append(pltpu.make_async_copy(ref, nat.at[slot], in_sem.at[slot]))
    field_loads = []
    for c in range(chunks):
        for t in range(tiles):
            field_loads.append(pltpu.make_async_copy(
                field.at[:, pl.ds(c * SUB, SUB), pl.ds(t * LANES, LANES)],
                rx.at[c, t].reshape(n, SUB, LANES), in_sem.at[6 + c * tiles + t]))
    for copy in loads + field_loads:
        copy.start()

    halo_r[...] = jnp.zeros_like(halo_r)
    barrier = pltpu.get_barrier_semaphore()
    for axis in (X, Y):
        for other in others(axis):
            pl.semaphore_signal(barrier, 1, device_id={names[axis]: other}, device_id_type=MESH)
    pl.semaphore_wait(barrier, parts_x + parts_y - 2)

    for copy in loads:
        copy.wait()
    for t in range(tiles):
        cols = pl.ds(t * LANES, LANES)
        pa[pl.ds(t, n, stride=pitch), :] = nat[0, :, cols]
        pb[pl.ds(t, n, stride=pitch), :] = nat[1, :, cols] + 1.0
        pc[pl.ds(t, n, stride=pitch), :] = nat[2, :, cols]
        for s in range(tiles):
            rows = pl.ds(s * LANES, LANES)
            dest = pl.ds(t * LANES * pitch + tiles + s, LANES, stride=pitch)
            pa[dest, :] = nat[3, rows, cols].T
            pb[dest, :] = nat[4, rows, cols].T + 1.0
            pc[dest, :] = nat[5, rows, cols].T

    unroll = 8
    zero = jnp.zeros((pitch, LANES), F32)
    one = jnp.ones((pitch, LANES), F32)

    def at_row(k, u):
        return pl.ds(pl.multiple_of(k * (unroll * pitch), unroll * pitch) + u * pitch, pitch)

    def pivots(g, state):
        dp, dq, c_prev, ep, eq, a_next = state
        h = n // unroll - 1 - g
        for u in range(unroll):
            up, down = at_row(g, u), at_row(h, unroll - 1 - u)
            nd[up, :] = dp
            new = pb[up, :] * dp - (pa[up, :] * c_prev) * dq
            md[up, :] = new
            dp, dq, c_prev = new, dp, pc[up, :]
            ne[down, :] = ep
            new = pb[down, :] * ep - (a_next * pc[down, :]) * eq
            me_[down, :] = new
            ep, eq, a_next = new, ep, pa[down, :]
            if u == unroll // 2 - 1:
                scale_d, scale_e = 1.0 / dp, 1.0 / ep
        return dp * scale_d, dq * scale_d, c_prev, ep * scale_e, eq * scale_e, a_next

    lax.fori_loop(0, n // unroll, pivots, (one, zero, zero, one, zero, zero))

    low_half = lax.broadcasted_iota(jnp.int32, (SUB, LANES), 0) < pitch
    blocks = n * pitch // SUB
    step_rows = 4

    def ratios(g, state):
        prev_m, next_d = state
        for u in range(step_rows):
            up = pl.ds(pl.multiple_of(g * (SUB * step_rows), SUB * step_rows) + u * SUB, SUB)
            down = pl.ds(pl.multiple_of((blocks // step_rows - 1 - g) * (SUB * step_rows), SUB * step_rows)
                         + (step_rows - 1 - u) * SUB, SUB)
            minv = nd[up, :] / md[up, :]
            m2[up, :] = minv + minv
            cn[up, :] = -pc[up, :] * minv
            turned = pltpu.roll(minv, pitch, 0)
            ln[up, :] = -pa[up, :] * jnp.where(low_half, prev_m, turned)
            prev_m = turned
            dinv = ne[down, :] / me_[down, :]
            d2[down, :] = dinv + dinv
            an[down, :] = -pa[down, :] * dinv
            turned = pltpu.roll(dinv, pitch, 0)
            un[down, :] = -pc[down, :] * jnp.where(low_half, turned, next_d)
            next_d = turned
        return prev_m, next_d

    blank = jnp.zeros((SUB, LANES), F32)
    lax.fori_loop(0, blocks // step_rows, ratios, (blank, blank))

    first, last = pl.ds(0, pitch), pl.ds((n - 1) * pitch, pitch)

    def products(g, state):
        col0, row0, coln, rown, un_prev, ln_next = state
        h = n // unroll - 1 - g
        for u in range(unroll):
            up, down = at_row(g, u), at_row(h, unroll - 1 - u)
            start = jnp.logical_and(g == 0, u == 0) if u == 0 else None
            f0, f1 = an[up, :], un_prev
            b0, b1 = cn[down, :], ln_next
            if u == 0:
                f0, f1 = jnp.where(start, one, f0), jnp.where(start, one, f1)
                b0, b1 = jnp.where(start, one, b0), jnp.where(start, one, b1)
            col0, row0, coln, rown = col0 * f0, row0 * f1, coln * b0, rown * b1
            w2[up, :], r0[up, :], v2[down, :], rn[down, :] = col0, row0, coln, rown
            un_prev, ln_next = un[up, :], ln[down, :]
        return col0, row0, coln, rown, un_prev, ln_next

    d_first, m_last = 0.5 * d2[first, :], 0.5 * m2[last, :]
    lax.fori_loop(0, n // unroll, products,
                  (-pa[first, :] * d2[first, :], d_first, -pc[last, :] * m2[last, :], m_last, one, one))

    for q, (ref, rows) in enumerate(((w2, first), (w2, last), (v2, first), (v2, last))):
        gs[pl.ds(q * pitch, pitch), :] = -0.5 * ref[rows, :]
    gathers = ((gsend_x, grecv_x), (gsend_y, grecv_y))
    for axis in (X, Y):
        gather[axis][pos[axis]] = gs[...]
        for off, other in enumerate(others(axis)):
            pltpu.make_async_remote_copy(
                src_ref=gs, dst_ref=gather[axis].at[pos[axis]], send_sem=gathers[axis][0].at[off],
                recv_sem=gathers[axis][1].at[pos[axis]], device_id={names[axis]: other}, device_id_type=MESH).start()

    def reduce_lines(axis):
        count, me = parts[axis], pos[axis]
        for off, other in enumerate(others(axis)):
            pltpu.make_async_remote_copy(
                src_ref=gs, dst_ref=gather[axis].at[other], send_sem=gathers[axis][0].at[off],
                recv_sem=gathers[axis][1].at[other], device_id={names[axis]: other}, device_id_type=MESH).wait()
        part = lambda p, q: gather[axis][p, pl.ds(q * pitch + axis * tiles, tiles), :]
        nil = jnp.zeros((tiles, LANES), F32)
        unit = jnp.ones((tiles, LANES), F32)
        mu, rho, tau = [None] * count, [None] * count, [None] * count
        prev = nil
        for p in range(count):
            wf, wt, vf, vt = (part(p, q) for q in range(4))
            kappa = 1.0 / (1.0 - wf * prev)
            mu[p], rho[p] = wt * prev * kappa, wt * kappa
            prev = tau[p] = vt + mu[p] * vf
        nu, omega, sigma = [None] * count, [None] * count, [None] * count
        prev = nil
        for p in reversed(range(count)):
            wf, wt, vf, vt = (part(p, q) for q in range(4))
            kappa = 1.0 / (1.0 - vt * prev)
            nu[p], omega[p] = vf * prev * kappa, vf * kappa
            prev = sigma[p] = wf + nu[p] * wt
        pick = lambda values, at: sum(jnp.where(at == p, v, nil) for p, v in enumerate(values))
        tau_b, sigma_a = pick(tau, me - 1), pick(sigma, me + 1)
        mu_me, nu_me = pick(mu, me), pick(nu, me)
        wf, wt, vf, vt = (part(me, q) for q in range(4))
        det = 1.0 / ((1.0 - tau_b * wf) * (1.0 - sigma_a * vt) - (tau_b * vf) * (sigma_a * wt))
        k11, k12 = (1.0 - sigma_a * vt) * det, tau_b * vf * det
        k21, k22 = sigma_a * wt * det, (1.0 - tau_b * wf) * det
        low, high = [None] * count, [None] * count
        for p in reversed(range(count)):
            onward = -rho[p + 1] * low[p + 1] if p + 1 < count else nil
            low[p] = jnp.where(me - 1 == p, unit, jnp.where(p < me - 1, onward, nil))
        for p in range(count):
            onward = -omega[p - 1] * high[p - 1] if p else nil
            high[p] = jnp.where(me + 1 == p, unit, jnp.where(p > me + 1, onward, nil))
        table = reduced[axis]
        put = lambda index, value: table.__setitem__((pl.ds(index * tiles, tiles), slice(None)), value)
        for p in range(count):
            put(p, k11 * low[p] + k12 * high[p] + jnp.where(me == p, -k11 * tau_b, nil))
            put(count + 1 + p, k21 * low[p] + k22 * high[p] + jnp.where(me == p, -k21 * tau_b, nil))
        put(count, -k12 * sigma_a)
        put(2 * count + 1, -k22 * sigma_a)
        put(2 * count + 2, mu_me)
        put(2 * count + 3, nu_me)

    def exchange(axis, stage, c, off, slot_here, other):
        sel = jnp.where(other > pos[axis], 1, 0)
        return pltpu.make_async_remote_copy(
            src_ref=send[axis].at[stage, c, sel], dst_ref=exch[axis].at[stage, c, slot_here],
            send_sem=send_sems[axis].at[stage, c, off], recv_sem=recv_sems[axis].at[stage, c, slot_here],
            device_id={names[axis]: other}, device_id_type=MESH)

    def publish(axis, stage, c):
        count, table = parts[axis], reduced[axis]
        for t in range(tiles):
            head, tail = exch[axis][stage, c, pos[axis], t], gt[c, t]
            mu = table[pl.ds((2 * count + 2) * tiles + t, 1), :]
            nu = table[pl.ds((2 * count + 3) * tiles + t, 1), :]
            send[axis][stage, c, 1, t] = tail + mu * head
            send[axis][stage, c, 0, t] = head + nu * tail
        for off, other in enumerate(others(axis)):
            exchange(axis, stage, c, off, pos[axis], other).start()

    def neighbours(axis, stage, c):
        count, table = parts[axis], reduced[axis]
        for off, other in enumerate(others(axis)):
            exchange(axis, stage, c, off, other, other).wait()
        for t in range(tiles):
            for side in range(2):
                base = side * (count + 1) * tiles + t
                total = table[pl.ds(base + count * tiles, 1), :] * gt[c, t]
                for p in range(count):
                    total = total + table[pl.ds(base + p * tiles, 1), :] * exch[axis][stage, c, p, t]
                ss[side, t] = total

    def turn(src, dst, c, axis, to, stage, correct, dots):
        def column(f, kt):
            heads = tails = None
            for lt in range(tiles):
                block = src[c, lt, pl.ds(kt * (LANES * SUB) + f, LANES, stride=SUB), :]
                if correct:
                    rows = pl.ds(kt * (LANES * pitch) + (axis * tiles + lt), LANES, stride=pitch)
                    block = (block + w2[rows, :] * ss[0, lt, pl.ds(f, 1), :]
                             + v2[rows, :] * ss[1, lt, pl.ds(f, 1), :])
                if dots is None:
                    block = block * 0.5
                flipped = block.T
                dst[c, kt, pl.ds(lt * LANES * SUB + f, LANES, stride=SUB), :] = flipped
                if dots:
                    rows = pl.ds(lt * LANES * pitch + to * tiles + kt, LANES, stride=pitch)
                    fold = lambda v: v.reshape(LANES // SUB, SUB, LANES).sum(axis=0)
                    h, s = fold(flipped * r0[rows, :]), fold(flipped * rn[rows, :])
                    heads = h if heads is None else heads + h
                    tails = s if tails is None else tails + s
            if dots:
                exch[to][stage, c, pos[to], kt, pl.ds(f, 1), :] = jnp.sum(heads, axis=0, keepdims=True)
                gt[c, kt, pl.ds(f, 1), :] = jnp.sum(tails, axis=0, keepdims=True)
            return kt

        lax.fori_loop(0, tiles, lambda kt, carry: (lax.fori_loop(0, SUB, column, kt, unroll=True), carry)[1], 0)

    cells = [(c, t) for c in range(chunks) for t in range(tiles)]

    def solve_block(ref, axis, minus):
        def coef(array, k, t):
            return array[pl.ds(k * pitch + axis * tiles + t, 1), :]

        def forward(k, state):
            ups, downs = list(state[0]), list(state[1])
            r = n - 1 - k
            for s, (c, t) in enumerate(cells):
                here = pl.ds(pl.multiple_of(k * SUB, SUB), SUB)
                ups[s] = ref[c, t, here, :] + coef(ln, k, t) * ups[s]
                hs[c, t, here, :] = ups[s]
                here = pl.ds(pl.multiple_of(r * SUB, SUB), SUB)
                downs[s] = ref[c, t, here, :] + coef(un, r, t) * downs[s]
                hs[c, t, here, :] = downs[s]
            return tuple(ups), tuple(downs)

        init = tuple(blank for _ in cells)
        ups, downs = lax.fori_loop(0, half, forward, (init, init), unroll=unroll)
        lo, hi = half - 1, half

        def place(c, t, k, value):
            here = pl.ds(pl.multiple_of(k * SUB, SUB), SUB)
            ref[c, t, here, :] = value - ref[c, t, here, :] if minus else value

        low_s, high_s = [], []
        for s, (c, t) in enumerate(cells):
            c_lo, a_hi = coef(cn, lo, t), coef(an, hi, t)
            kappa = 1.0 / (1.0 - c_lo * a_hi)
            h_hi = coef(d2, hi, t) * downs[s]
            s_lo = kappa * (coef(m2, lo, t) * ups[s] + c_lo * h_hi)
            low_s.append(s_lo)
            high_s.append(h_hi + a_hi * s_lo)
            place(c, t, lo, low_s[s])
            place(c, t, hi, high_s[s])

        def backward(step, state):
            lows, highs = list(state[0]), list(state[1])
            k, r = half - 1 - step, half + step
            for s, (c, t) in enumerate(cells):
                here = pl.ds(pl.multiple_of(k * SUB, SUB), SUB)
                lows[s] = coef(m2, k, t) * hs[c, t, here, :] + coef(cn, k, t) * lows[s]
                place(c, t, k, lows[s])
                here = pl.ds(pl.multiple_of(r * SUB, SUB), SUB)
                highs[s] = coef(d2, r, t) * hs[c, t, here, :] + coef(an, r, t) * highs[s]
                place(c, t, r, highs[s])
            return tuple(lows), tuple(highs)

        state = lax.fori_loop(1, unroll, backward, (tuple(low_s), tuple(high_s)), unroll=True)
        lax.fori_loop(unroll, half, backward, state, unroll=unroll)

    for copy in field_loads:
        copy.wait()
    lax.fori_loop(0, chunks, lambda c, carry: (turn(rx, ry, c, X, Y, 0, False, False), carry)[1], 0)
    me_y = pos[Y]
    tail_rows = pl.ds((n - 1) * SUB, SUB)
    for c, t in cells:
        halo_s[0, c, t] = ry[c, t, pl.ds(0, SUB), :]
        halo_s[1, c, t] = ry[c, t, tail_rows, :]

    def halo(side, other):
        return pltpu.make_async_remote_copy(
            src_ref=halo_s.at[side], dst_ref=halo_r.at[1 - side], send_sem=hsend.at[side], recv_sem=hrecv.at[1 - side],
            device_id={col_name: other}, device_id_type=MESH)

    has_before, has_after = me_y > 0, me_y < parts_y - 1

    @pl.when(has_before)
    def _():
        halo(0, me_y - 1).start()

    @pl.when(has_after)
    def _():
        halo(1, me_y + 1).start()

    def explicit(k, state):
        befores, heres = list(state[0]), list(state[1])
        coef = lambda array, t: array[pl.ds(k * pitch + tiles + t, 1), :]
        for s, (c, t) in enumerate(cells):
            ahead = ry[c, t, pl.ds(pl.multiple_of(jnp.minimum(k + 1, n - 1) * SUB, SUB), SUB), :]
            ahead = jnp.where(k == n - 1, blank, ahead)
            ry[c, t, pl.ds(pl.multiple_of(k * SUB, SUB), SUB), :] = heres[s] - (
                coef(pa, t) * befores[s] + (coef(pb, t) - 1.0) * heres[s] + coef(pc, t) * ahead)
            befores[s], heres[s] = heres[s], ahead
        return tuple(befores), tuple(heres)

    lax.fori_loop(0, n, explicit,
                  (tuple(blank for _ in cells), tuple(ry[c, t, pl.ds(0, SUB), :] for c, t in cells)), unroll=unroll)

    @pl.when(has_before)
    def _():
        halo(0, me_y - 1).wait_send()
        halo(1, me_y - 1).wait_recv()

    @pl.when(has_after)
    def _():
        halo(1, me_y + 1).wait_send()
        halo(0, me_y + 1).wait_recv()

    for c, t in cells:
        ry[c, t, pl.ds(0, SUB), :] = ry[c, t, pl.ds(0, SUB), :] - pa[pl.ds(tiles + t, 1), :] * halo_r[0, c, t]
        ry[c, t, tail_rows, :] = (ry[c, t, tail_rows, :]
                                  - pc[pl.ds((n - 1) * pitch + tiles + t, 1), :] * halo_r[1, c, t])

    def each_chunk(body):
        lax.fori_loop(0, chunks, lambda c, carry: (body(c), carry)[1], 0)

    def start_x(c):
        turn(ry, rx, c, Y, X, 0, False, True)
        publish(X, 0, c)

    reduce_lines(X)
    each_chunk(start_x)
    reduce_lines(Y)

    def x_half(stage):
        def finish(c):
            neighbours(X, stage, c)
            turn(rx, ry, c, X, Y, stage, True, True)
            publish(Y, stage, c)

        solve_block(rx, X, True)
        each_chunk(finish)

    def step(stage, carry):
        def finish(c):
            neighbours(Y, stage, c)
            turn(ry, rx, c, Y, X, stage + 1, True, True)
            publish(X, stage + 1, c)

        x_half(stage)
        solve_block(ry, Y, True)
        each_chunk(finish)
        return carry

    lax.fori_loop(0, STEPS - 1, step, 0)
    x_half(STEPS - 1)
    solve_block(ry, Y, False)
    for c in range(chunks):
        neighbours(Y, STEPS - 1, c)
        turn(ry, rx, c, Y, X, STEPS, True, None)
        for t in range(tiles):
            pltpu.make_async_copy(rx.at[c, t].reshape(n, SUB, LANES),
                                  out.at[:, pl.ds(c * SUB, SUB), pl.ds(t * LANES, LANES)],
                                  out_sem.at[c * tiles + t]).start()
    for c, t in cells:
        pltpu.make_async_copy(rx.at[c, t].reshape(n, SUB, LANES),
                              out.at[:, pl.ds(c * SUB, SUB), pl.ds(t * LANES, LANES)],
                              out_sem.at[c * tiles + t]).wait()


def solution(mesh):
    parts_x, parts_y = mesh.shape["row"], mesh.shape["col"]
    field_spec = P(("batch", "row"), "col", None)
    coeff_spec = P(("batch", "row"), "col")

    def local_steps(field, *coeffs):
        n, fields = field.shape[0], field.shape[2]
        tiles, chunks = n // LANES, fields // SUB
        packed = pltpu.VMEM((n * 2 * tiles, LANES), F32)
        big = pltpu.VMEM((chunks, tiles, n * SUB, LANES), F32)
        dma = pltpu.SemaphoreType.DMA
        line = lambda count: pltpu.VMEM((STEPS, chunks, count, tiles, SUB, LANES), F32)
        table = lambda count: pltpu.VMEM(((2 * count + 4) * tiles, LANES), F32)
        small = pltpu.VMEM((2, chunks, tiles, SUB, LANES), F32)
        message = (8 * tiles, LANES)
        scratch = [
            pltpu.VMEM((6, n, n), F32), big, big, big, *([packed] * 17),
            pltpu.VMEM(message, F32), pltpu.VMEM((parts_x,) + message, F32), pltpu.VMEM((parts_y,) + message, F32),
            table(parts_x), table(parts_y), line(2), line(2), line(parts_x), line(parts_y),
            pltpu.VMEM((chunks, tiles, SUB, LANES), F32), pltpu.VMEM((2, tiles, SUB, LANES), F32), small, small,
            dma((6 + chunks * tiles,)), dma((chunks * tiles,)), dma((parts_x,)), dma((parts_y,)), dma((parts_x,)), dma((parts_y,)),
            dma((STEPS, chunks, parts_x)), dma((STEPS, chunks, parts_y)),
            dma((STEPS, chunks, parts_x)), dma((STEPS, chunks, parts_y)), dma((2,)), dma((2,)),
        ]
        anywhere = pl.BlockSpec(memory_space=pl.ANY)
        turned = jnp.transpose(field, (0, 2, 1))
        result = pl.pallas_call(
            functools.partial(adi_kernel, (("row", parts_x), ("col", parts_y))),
            out_shape=jax.ShapeDtypeStruct(turned.shape, F32),
            in_specs=[anywhere] * 7, out_specs=anywhere, scratch_shapes=scratch,
            compiler_params=pltpu.CompilerParams(collective_id=0, has_side_effects=True, vmem_limit_bytes=48 * 1024 * 1024),
            name="adi_steps",
        )(turned, *coeffs)
        return jnp.transpose(result, (0, 2, 1))

    return jax.shard_map(local_steps, mesh=mesh, in_specs=(field_spec,) + (coeff_spec,) * 6, out_specs=field_spec, check_vma=False)
```

profile of v0, /device:TPU:97, one launch (start us, length us, event | category | flops | bytes accessed | tf_op | source)
XLA Modules:
  0.0 62.7 jit_solution(8264539544103588620)
XLA Ops:
  0.0 0.0 copy-start
  0.0 0.9 %copy-done = f32[256,256]{1,0:T(8,128)S(1)} copy-done((f32[256,256]{1,0:T(8,128)S(1)}, f32[256,256]{1,0:T(8,128)}, u32[]{:S(2)}) %copy-start) | copy-done | bytes 262168
  1.0 0.0 copy-start.1
  1.0 0.9 %copy-done.1 = f32[256,256]{1,0:T(8,128)S(1)} copy-done((f32[256,256]{1,0:T(8,128)S(1)}, f32[256,256]{1,0:T(8,128)}, u32[]{:S(2)}) %copy-start.1) | copy-done | bytes 262168
  1.9 0.0 copy-start.2
  1.9 0.9 %copy-done.2 = f32[256,256]{1,0:T(8,128)S(1)} copy-done((f32[256,256]{1,0:T(8,128)S(1)}, f32[256,256]{1,0:T(8,128)}, u32[]{:S(2)}) %copy-start.2) | copy-done | bytes 262168
  2.9 0.0 copy-start.3
  2.9 0.9 %copy-done.3 = f32[256,256]{1,0:T(8,128)S(1)} copy-done((f32[256,256]{1,0:T(8,128)S(1)}, f32[256,256]{1,0:T(8,128)}, u32[]{:S(2)}) %copy-start.3) | copy-done | bytes 262168
  3.8 0.0 copy-start.4
  3.8 0.9 %copy-done.4 = f32[256,256]{1,0:T(8,128)S(1)} copy-done((f32[256,256]{1,0:T(8,128)S(1)}, f32[256,256]{1,0:T(8,128)}, u32[]{:S(2)}) %copy-start.4) | copy-done | bytes 262168
  4.8 0.0 copy-start.5
  4.8 0.9 %copy-done.5 = f32[256,256]{1,0:T(8,128)S(1)} copy-done((f32[256,256]{1,0:T(8,128)S(1)}, f32[256,256]{1,0:T(8,128)}, u32[]{:S(2)}) %copy-start.5) | copy-done | bytes 262168
  5.7 55.0 %adi_steps.1 = f32[256,16,256]{2,1,0:T(8,128)S(1)} custom-call(f32[256,16,256]{2,1,0:T(8,128)} %bitcast.3, f32[256,256]{1,0:T(8,128)S(1)} %copy-done, f32[256,256]{1,0:T(8,128)S(1)} %copy-done.1, f32[256,256]{1,0:T(8,128)S(1)} %copy-done.2, f32[256,256]{1,0:T(8,128)S(1)} %copy-done.3, f32[256,256]{1,0:T(8,128)S(1)} %copy-done.4, f32[256,256]{1,0:T(8,128)S(1)} %copy-done.5), custom_call_target="tpu_custom_call" | custom-call | tf_op jit(solution)/shard_map/adi_steps/pallas_call | solution.py:440
  60.7 2.0 %copy.9 = f32[256,256,16]{1,2,0:T(8,128)} copy(f32[256,256,16]{1,2,0:T(8,128)S(1)} %bitcast.2) | data formatting | bytes 8388608
Async XLA Ops:
  0.0 0.9 %copy-start = (f32[256,256]{1,0:T(8,128)S(1)}, f32[256,256]{1,0:T(8,128)}, u32[]{:S(2)}) copy-start(f32[256,256]{1,0:T(8,128)} %lower_x.1) | copy-start | bytes 786436
  1.0 0.9 %copy-start.1 = (f32[256,256]{1,0:T(8,128)S(1)}, f32[256,256]{1,0:T(8,128)}, u32[]{:S(2)}) copy-start(f32[256,256]{1,0:T(8,128)} %diag_x.1) | copy-start | bytes 786436
  1.9 0.9 %copy-start.2 = (f32[256,256]{1,0:T(8,128)S(1)}, f32[256,256]{1,0:T(8,128)}, u32[]{:S(2)}) copy-start(f32[256,256]{1,0:T(8,128)} %upper_x.1) | copy-start | bytes 786436
  2.9 0.9 %copy-start.3 = (f32[256,256]{1,0:T(8,128)S(1)}, f32[256,256]{1,0:T(8,128)}, u32[]{:S(2)}) copy-start(f32[256,256]{1,0:T(8,128)} %lower_y.1) | copy-start | bytes 786436
  3.8 0.9 %copy-start.4 = (f32[256,256]{1,0:T(8,128)S(1)}, f32[256,256]{1,0:T(8,128)}, u32[]{:S(2)}) copy-start(f32[256,256]{1,0:T(8,128)} %diag_y.1) | copy-start | bytes 786436
  4.8 0.9 %copy-start.5 = (f32[256,256]{1,0:T(8,128)S(1)}, f32[256,256]{1,0:T(8,128)}, u32[]{:S(2)}) copy-start(f32[256,256]{1,0:T(8,128)} %upper_y.1) | copy-start | bytes 786436
where the time goes:
time: 63 us; the launch traced here: 62.7 us
  Pallas kernels  55 us (87%)
  local copies, waits for them, and re-layouts  7.71 us (12%)
    pallas_call x1, Pallas kernels, local_steps(): pl.pallas_call(functools.partial(adi_kernel, (('row', parts_x), ('col', p...  55 us
    unnamed x13, local copies, waits for them, and re-layouts  7.71 us

commit v1 on v0

--- a/solution.py
+++ b/solution.py
@@ -11,14 +11,15 @@
 F32 = jnp.float32
 LANES = 128
 SUB = 8
+PITCH = SUB + 1
 MESH = pl.DeviceIdType.MESH
 X, Y = 0, 1
 
 
 def adi_kernel(axes, field, lower_x, diag_x, upper_x, lower_y, diag_y, upper_y, out,
-               nat, rx, ry, hs, pa, pb, pc, nd, md, ne, me_, ln, cn, un, an, m2, d2, w2, v2, r0, rn,
+               nat, stage_in, rs, hs, qs, pa, pb, pc, nd, md, ne, me_, ln, cn, un, an, m2, d2, w2, v2, r0, rn,
                gs, gc_x, gc_y, red_x, red_y, sx, sy, ex, ey, gt, ss, halo_s, halo_r,
-               in_sem, out_sem, gsend_x, gsend_y, grecv_x, grecv_y, ssx, ssy, rsx, rsy, hsend, hrecv):
+               coef_sem, field_sem, gsend, grecv, send_sem, recv_sem, hsend, hrecv):
     (row_name, parts_x), (col_name, parts_y) = axes
     n = lower_x.shape[0]
     tiles = n // LANES
@@ -30,35 +31,26 @@
     names = (row_name, col_name)
     exch = (ex, ey)
     send = (sx, sy)
-    send_sems = (ssx, ssy)
-    recv_sems = (rsx, rsy)
     gather = (gc_x, gc_y)
     reduced = (red_x, red_y)
 
     def others(axis):
         return [lax.rem(pos[axis] + off, parts[axis]) for off in range(1, parts[axis])]
 
-    loads = []
     for slot, ref in enumerate((lower_x, diag_x, upper_x, lower_y, diag_y, upper_y)):
-        loads.append(pltpu.make_async_copy(ref, nat.at[slot], in_sem.at[slot]))
-    field_loads = []
+        pltpu.make_async_copy(ref, nat.at[slot], coef_sem).start()
     for c in range(chunks):
         for t in range(tiles):
-            field_loads.append(pltpu.make_async_copy(
-                field.at[:, pl.ds(c * SUB, SUB), pl.ds(t * LANES, LANES)],
-                rx.at[c, t].reshape(n, SUB, LANES), in_sem.at[6 + c * tiles + t]))
-    for copy in loads + field_loads:
-        copy.start()
+            pltpu.make_async_copy(field.at[:, pl.ds(c * SUB, SUB), pl.ds(t * LANES, LANES)],
+                                  stage_in.at[c, t].reshape(n, SUB, LANES), field_sem).start()
 
     halo_r[...] = jnp.zeros_like(halo_r)
     barrier = pltpu.get_barrier_semaphore()
     for axis in (X, Y):
         for other in others(axis):
             pl.semaphore_signal(barrier, 1, device_id={names[axis]: other}, device_id_type=MESH)
-    pl.semaphore_wait(barrier, parts_x + parts_y - 2)
-
-    for copy in loads:
-        copy.wait()
+
+    pltpu.make_async_copy(nat, nat, coef_sem).wait()
     for t in range(tiles):
         cols = pl.ds(t * LANES, LANES)
         pa[pl.ds(t, n, stride=pitch), :] = nat[0, :, cols]
@@ -148,20 +140,18 @@
 
     for q, (ref, rows) in enumerate(((w2, first), (w2, last), (v2, first), (v2, last))):
         gs[pl.ds(q * pitch, pitch), :] = -0.5 * ref[rows, :]
-    gathers = ((gsend_x, grecv_x), (gsend_y, grecv_y))
+    pl.semaphore_wait(barrier, parts_x + parts_y - 2)
     for axis in (X, Y):
         gather[axis][pos[axis]] = gs[...]
-        for off, other in enumerate(others(axis)):
+        for other in others(axis):
             pltpu.make_async_remote_copy(
-                src_ref=gs, dst_ref=gather[axis].at[pos[axis]], send_sem=gathers[axis][0].at[off],
-                recv_sem=gathers[axis][1].at[pos[axis]], device_id={names[axis]: other}, device_id_type=MESH).start()
+                src_ref=gs, dst_ref=gather[axis].at[pos[axis]], send_sem=gsend, recv_sem=grecv.at[axis],
+                device_id={names[axis]: other}, device_id_type=MESH).start()
 
     def reduce_lines(axis):
         count, me = parts[axis], pos[axis]
-        for off, other in enumerate(others(axis)):
-            pltpu.make_async_remote_copy(
-                src_ref=gs, dst_ref=gather[axis].at[other], send_sem=gathers[axis][0].at[off],
-                recv_sem=gathers[axis][1].at[other], device_id={names[axis]: other}, device_id_type=MESH).wait()
+        arrived = gather[axis].at[pl.ds(0, count - 1)]
+        pltpu.make_async_copy(arrived, arrived, grecv.at[axis]).wait()
         part = lambda p, q: gather[axis][p, pl.ds(q * pitch + axis * tiles, tiles), :]
         nil = jnp.zeros((tiles, LANES), F32)
         unit = jnp.ones((tiles, LANES), F32)
@@ -203,41 +193,41 @@
         put(2 * count + 2, mu_me)
         put(2 * count + 3, nu_me)
 
-    def exchange(axis, stage, c, off, slot_here, other):
-        sel = jnp.where(other > pos[axis], 1, 0)
-        return pltpu.make_async_remote_copy(
-            src_ref=send[axis].at[stage, c, sel], dst_ref=exch[axis].at[stage, c, slot_here],
-            send_sem=send_sems[axis].at[stage, c, off], recv_sem=recv_sems[axis].at[stage, c, slot_here],
-            device_id={names[axis]: other}, device_id_type=MESH)
-
     def publish(axis, stage, c):
-        count, table = parts[axis], reduced[axis]
+        count, table, way = parts[axis], reduced[axis], lax.rem(stage, 2)
         for t in range(tiles):
-            head, tail = exch[axis][stage, c, pos[axis], t], gt[c, t]
+            head, tail = exch[axis][way, c, pos[axis], t], gt[c, t]
             mu = table[pl.ds((2 * count + 2) * tiles + t, 1), :]
             nu = table[pl.ds((2 * count + 3) * tiles + t, 1), :]
-            send[axis][stage, c, 1, t] = tail + mu * head
-            send[axis][stage, c, 0, t] = head + nu * tail
-        for off, other in enumerate(others(axis)):
-            exchange(axis, stage, c, off, pos[axis], other).start()
+            send[axis][c, 1, t] = tail + mu * head
+            send[axis][c, 0, t] = head + nu * tail
+        for other in others(axis):
+            sel = jnp.where(other > pos[axis], 1, 0)
+            pltpu.make_async_remote_copy(
+                src_ref=send[axis].at[c, sel], dst_ref=exch[axis].at[way, c, pos[axis]],
+                send_sem=send_sem.at[axis, c], recv_sem=recv_sem.at[axis, way, c],
+                device_id={names[axis]: other}, device_id_type=MESH).start()
 
     def neighbours(axis, stage, c):
-        count, table = parts[axis], reduced[axis]
-        for off, other in enumerate(others(axis)):
-            exchange(axis, stage, c, off, other, other).wait()
+        count, table, way = parts[axis], reduced[axis], lax.rem(stage, 2)
+        arrived = exch[axis].at[way, c, pl.ds(0, count - 1)]
+        pltpu.make_async_copy(arrived, arrived, recv_sem.at[axis, way, c]).wait()
+        pltpu.make_async_copy(arrived, arrived, send_sem.at[axis, c]).wait()
         for t in range(tiles):
             for side in range(2):
                 base = side * (count + 1) * tiles + t
                 total = table[pl.ds(base + count * tiles, 1), :] * gt[c, t]
                 for p in range(count):
-                    total = total + table[pl.ds(base + p * tiles, 1), :] * exch[axis][stage, c, p, t]
+                    total = total + table[pl.ds(base + p * tiles, 1), :] * exch[axis][way, c, p, t]
                 ss[side, t] = total
 
-    def turn(src, dst, c, axis, to, stage, correct, dots):
+    def turn(src, dst, c, axis, to, stage, correct, dots, step_in=PITCH):
+        way = lax.rem(stage, 2)
+
         def column(f, kt):
             heads = tails = None
             for lt in range(tiles):
-                block = src[c, lt, pl.ds(kt * (LANES * SUB) + f, LANES, stride=SUB), :]
+                block = src[c, lt, pl.ds(kt * (LANES * step_in) + f, LANES, stride=step_in), :]
                 if correct:
                     rows = pl.ds(kt * (LANES * pitch) + (axis * tiles + lt), LANES, stride=pitch)
                     block = (block + w2[rows, :] * ss[0, lt, pl.ds(f, 1), :]
@@ -245,7 +235,7 @@
                 if dots is None:
                     block = block * 0.5
                 flipped = block.T
-                dst[c, kt, pl.ds(lt * LANES * SUB + f, LANES, stride=SUB), :] = flipped
+                dst[c, kt, pl.ds(lt * LANES * PITCH + f, LANES, stride=PITCH), :] = flipped
                 if dots:
                     rows = pl.ds(lt * LANES * pitch + to * tiles + kt, LANES, stride=pitch)
                     fold = lambda v: v.reshape(LANES // SUB, SUB, LANES).sum(axis=0)
@@ -253,7 +243,7 @@
                     heads = h if heads is None else heads + h
                     tails = s if tails is None else tails + s
             if dots:
-                exch[to][stage, c, pos[to], kt, pl.ds(f, 1), :] = jnp.sum(heads, axis=0, keepdims=True)
+                exch[to][way, c, pos[to], kt, pl.ds(f, 1), :] = jnp.sum(heads, axis=0, keepdims=True)
                 gt[c, kt, pl.ds(f, 1), :] = jnp.sum(tails, axis=0, keepdims=True)
             return kt
 
@@ -261,7 +251,10 @@
 
     cells = [(c, t) for c in range(chunks) for t in range(tiles)]
 
-    def solve_block(ref, axis, minus):
+    def slab(k):
+        return pl.ds(k * PITCH, SUB)
+
+    def solve_block(axis, minus):
         def coef(array, k, t):
             return array[pl.ds(k * pitch + axis * tiles + t, 1), :]
 
@@ -269,12 +262,10 @@
             ups, downs = list(state[0]), list(state[1])
             r = n - 1 - k
             for s, (c, t) in enumerate(cells):
-                here = pl.ds(pl.multiple_of(k * SUB, SUB), SUB)
-                ups[s] = ref[c, t, here, :] + coef(ln, k, t) * ups[s]
-                hs[c, t, here, :] = ups[s]
-                here = pl.ds(pl.multiple_of(r * SUB, SUB), SUB)
-                downs[s] = ref[c, t, here, :] + coef(un, r, t) * downs[s]
-                hs[c, t, here, :] = downs[s]
+                ups[s] = rs[c, t, slab(k), :] + coef(ln, k, t) * ups[s]
+                hs[c, t, slab(k), :] = ups[s]
+                downs[s] = rs[c, t, slab(r), :] + coef(un, r, t) * downs[s]
+                hs[c, t, slab(r), :] = downs[s]
             return tuple(ups), tuple(downs)
 
         init = tuple(blank for _ in cells)
@@ -282,8 +273,7 @@
         lo, hi = half - 1, half
 
         def place(c, t, k, value):
-            here = pl.ds(pl.multiple_of(k * SUB, SUB), SUB)
-            ref[c, t, here, :] = value - ref[c, t, here, :] if minus else value
+            qs[c, t, slab(k), :] = value - rs[c, t, slab(k), :] if minus else value
 
         low_s, high_s = [], []
         for s, (c, t) in enumerate(cells):
@@ -300,25 +290,24 @@
             lows, highs = list(state[0]), list(state[1])
             k, r = half - 1 - step, half + step
             for s, (c, t) in enumerate(cells):
-                here = pl.ds(pl.multiple_of(k * SUB, SUB), SUB)
-                lows[s] = coef(m2, k, t) * hs[c, t, here, :] + coef(cn, k, t) * lows[s]
+                lows[s] = coef(m2, k, t) * hs[c, t, slab(k), :] + coef(cn, k, t) * lows[s]
                 place(c, t, k, lows[s])
-                here = pl.ds(pl.multiple_of(r * SUB, SUB), SUB)
-                highs[s] = coef(d2, r, t) * hs[c, t, here, :] + coef(an, r, t) * highs[s]
+                highs[s] = coef(d2, r, t) * hs[c, t, slab(r), :] + coef(an, r, t) * highs[s]
                 place(c, t, r, highs[s])
             return tuple(lows), tuple(highs)
 
         state = lax.fori_loop(1, unroll, backward, (tuple(low_s), tuple(high_s)), unroll=True)
         lax.fori_loop(unroll, half, backward, state, unroll=unroll)
 
-    for copy in field_loads:
-        copy.wait()
-    lax.fori_loop(0, chunks, lambda c, carry: (turn(rx, ry, c, X, Y, 0, False, False), carry)[1], 0)
+    def each_chunk(body):
+        lax.fori_loop(0, chunks, lambda c, carry: (body(c), carry)[1], 0)
+
+    pltpu.make_async_copy(stage_in, stage_in, field_sem).wait()
+    each_chunk(lambda c: turn(stage_in, rs, c, X, Y, 0, False, False, SUB))
     me_y = pos[Y]
-    tail_rows = pl.ds((n - 1) * SUB, SUB)
     for c, t in cells:
-        halo_s[0, c, t] = ry[c, t, pl.ds(0, SUB), :]
-        halo_s[1, c, t] = ry[c, t, tail_rows, :]
+        halo_s[0, c, t] = rs[c, t, slab(0), :]
+        halo_s[1, c, t] = rs[c, t, slab(n - 1), :]
 
     def halo(side, other):
         return pltpu.make_async_remote_copy(
@@ -339,15 +328,14 @@
         befores, heres = list(state[0]), list(state[1])
         coef = lambda array, t: array[pl.ds(k * pitch + tiles + t, 1), :]
         for s, (c, t) in enumerate(cells):
-            ahead = ry[c, t, pl.ds(pl.multiple_of(jnp.minimum(k + 1, n - 1) * SUB, SUB), SUB), :]
-            ahead = jnp.where(k == n - 1, blank, ahead)
-            ry[c, t, pl.ds(pl.multiple_of(k * SUB, SUB), SUB), :] = heres[s] - (
-                coef(pa, t) * befores[s] + (coef(pb, t) - 1.0) * heres[s] + coef(pc, t) * ahead)
+            ahead = rs[c, t, slab(k + 1), :]
+            qs[c, t, slab(k), :] = (2.0 - coef(pb, t)) * heres[s] - (coef(pa, t) * befores[s] + coef(pc, t) * ahead)
             befores[s], heres[s] = heres[s], ahead
         return tuple(befores), tuple(heres)
 
-    lax.fori_loop(0, n, explicit,
-                  (tuple(blank for _ in cells), tuple(ry[c, t, pl.ds(0, SUB), :] for c, t in cells)), unroll=unroll)
+    befores, heres = lax.fori_loop(
+        0, n - unroll, explicit, (tuple(blank for _ in cells), tuple(rs[c, t, slab(0), :] for c, t in cells)), unroll=unroll)
+    befores, heres = lax.fori_loop(n - unroll, n - 1, explicit, (befores, heres), unroll=True)
 
     @pl.when(has_before)
     def _():
@@ -359,56 +347,59 @@
         halo(1, me_y + 1).wait_send()
         halo(0, me_y + 1).wait_recv()
 
-    for c, t in cells:
-        ry[c, t, pl.ds(0, SUB), :] = ry[c, t, pl.ds(0, SUB), :] - pa[pl.ds(tiles + t, 1), :] * halo_r[0, c, t]
-        ry[c, t, tail_rows, :] = (ry[c, t, tail_rows, :]
-                                  - pc[pl.ds((n - 1) * pitch + tiles + t, 1), :] * halo_r[1, c, t])
-
-    def each_chunk(body):
-        lax.fori_loop(0, chunks, lambda c, carry: (body(c), carry)[1], 0)
+    for s, (c, t) in enumerate(cells):
+        here = pl.ds((n - 1) * pitch + tiles + t, 1)
+        qs[c, t, slab(n - 1), :] = (2.0 - pb[here, :]) * heres[s] - (pa[here, :] * befores[s] + pc[here, :] * halo_r[1, c, t])
+        qs[c, t, slab(0), :] = qs[c, t, slab(0), :] - pa[pl.ds(tiles + t, 1), :] * halo_r[0, c, t]
 
     def start_x(c):
-        turn(ry, rx, c, Y, X, 0, False, True)
+        turn(qs, rs, c, Y, X, 0, False, True)
         publish(X, 0, c)
 
     reduce_lines(X)
     each_chunk(start_x)
     reduce_lines(Y)
+    sent = gc_x.at[pl.ds(0, parts_x - 1)]
+    pltpu.make_async_copy(sent, sent, gsend).wait()
+    sent = gc_y.at[pl.ds(0, parts_y - 1)]
+    pltpu.make_async_copy(sent, sent, gsend).wait()
 
     def x_half(stage):
         def finish(c):
             neighbours(X, stage, c)
-            turn(rx, ry, c, X, Y, stage, True, True)
+            turn(qs, rs, c, X, Y, stage, True, True)
             publish(Y, stage, c)
 
-        solve_block(rx, X, True)
+        solve_block(X, True)
         each_chunk(finish)
 
     def step(stage, carry):
         def finish(c):
             neighbours(Y, stage, c)
-            turn(ry, rx, c, Y, X, stage + 1, True, True)
+            turn(qs, rs, c, Y, X, stage + 1, True, True)
             publish(X, stage + 1, c)
 
         x_half(stage)
-        solve_block(ry, Y, True)
+        solve_block(Y, True)
         each_chunk(finish)
         return carry
 
     lax.fori_loop(0, STEPS - 1, step, 0)
     x_half(STEPS - 1)
-    solve_block(ry, Y, False)
-    for c in range(chunks):
+    solve_block(Y, False)
+
+    def finish(c):
         neighbours(Y, STEPS - 1, c)
-        turn(ry, rx, c, Y, X, STEPS, True, None)
-        for t in range(tiles):
-            pltpu.make_async_copy(rx.at[c, t].reshape(n, SUB, LANES),
-                                  out.at[:, pl.ds(c * SUB, SUB), pl.ds(t * LANES, LANES)],
-                                  out_sem.at[c * tiles + t]).start()
-    for c, t in cells:
-        pltpu.make_async_copy(rx.at[c, t].reshape(n, SUB, LANES),
-                              out.at[:, pl.ds(c * SUB, SUB), pl.ds(t * LANES, LANES)],
-                              out_sem.at[c * tiles + t]).wait()
+        turn(qs, rs, c, Y, X, STEPS, True, None)
+
+        def unload(k, carry):
+            for t in range(tiles):
+                out[k, pl.ds(pl.multiple_of(c * SUB, SUB), SUB), pl.ds(t * LANES, LANES)] = rs[c, t, slab(k), :]
+            return carry
+
+        lax.fori_loop(0, n, unload, 0, unroll=unroll)
+
+    each_chunk(finish)
 
 
 def solution(mesh):
@@ -420,30 +411,29 @@
         n, fields = field.shape[0], field.shape[2]
         tiles, chunks = n // LANES, fields // SUB
         packed = pltpu.VMEM((n * 2 * tiles, LANES), F32)
-        big = pltpu.VMEM((chunks, tiles, n * SUB, LANES), F32)
+        big = pltpu.VMEM((chunks, tiles, n * PITCH, LANES), F32)
         dma = pltpu.SemaphoreType.DMA
-        line = lambda count: pltpu.VMEM((STEPS, chunks, count, tiles, SUB, LANES), F32)
+        sends = pltpu.VMEM((chunks, 2, tiles, SUB, LANES), F32)
+        line = lambda count: pltpu.VMEM((2, chunks, count, tiles, SUB, LANES), F32)
         table = lambda count: pltpu.VMEM(((2 * count + 4) * tiles, LANES), F32)
         small = pltpu.VMEM((2, chunks, tiles, SUB, LANES), F32)
         message = (8 * tiles, LANES)
         scratch = [
-            pltpu.VMEM((6, n, n), F32), big, big, big, *([packed] * 17),
+            pltpu.VMEM((6, n, n), F32), pltpu.VMEM((chunks, tiles, n * SUB, LANES), F32), big, big, big, *([packed] * 17),
             pltpu.VMEM(message, F32), pltpu.VMEM((parts_x,) + message, F32), pltpu.VMEM((parts_y,) + message, F32),
-            table(parts_x), table(parts_y), line(2), line(2), line(parts_x), line(parts_y),
+            table(parts_x), table(parts_y), sends, sends, line(parts_x), line(parts_y),
             pltpu.VMEM((chunks, tiles, SUB, LANES), F32), pltpu.VMEM((2, tiles, SUB, LANES), F32), small, small,
-            dma((6 + chunks * tiles,)), dma((chunks * tiles,)), dma((parts_x,)), dma((parts_y,)), dma((parts_x,)), dma((parts_y,)),
-            dma((STEPS, chunks, parts_x)), dma((STEPS, chunks, parts_y)),
-            dma((STEPS, chunks, parts_x)), dma((STEPS, chunks, parts_y)), dma((2,)), dma((2,)),
+            dma, dma, dma, dma((2,)), dma((2, chunks)), dma((2, 2, chunks)), dma((2,)), dma((2,)),
         ]
-        anywhere = pl.BlockSpec(memory_space=pl.ANY)
+        in_hbm = pl.BlockSpec(memory_space=pltpu.HBM)
         turned = jnp.transpose(field, (0, 2, 1))
         result = pl.pallas_call(
             functools.partial(adi_kernel, (("row", parts_x), ("col", parts_y))),
             out_shape=jax.ShapeDtypeStruct(turned.shape, F32),
-            in_specs=[anywhere] * 7, out_specs=anywhere, scratch_shapes=scratch,
+            in_specs=[in_hbm] * 7, out_specs=pl.BlockSpec(memory_space=pltpu.VMEM), scratch_shapes=scratch,
             compiler_params=pltpu.CompilerParams(collective_id=0, has_side_effects=True, vmem_limit_bytes=48 * 1024 * 1024),
             name="adi_steps",
-        )(turned, *coeffs)
+        )(turned, *(pltpu.with_memory_space_constraint(array, pltpu.HBM) for array in coeffs))
         return jnp.transpose(result, (0, 2, 1))
 
     return jax.shard_map(local_steps, mesh=mesh, in_specs=(field_spec,) + (coeff_spec,) * 6, out_specs=field_spec, check_vma=False)

time: 63 us -> 45 us (0.71)
  Pallas kernels: 55 us -> 42.9 us
  local copies, waits for them, and re-layouts: 7.71 us -> 2.02 us
    pallas_call x1, Pallas kernels: 55 us -> 42.9 us  [local_steps(): pl.pallas_call(functools.partial(adi_kernel, (('row', parts_x), ('col', p...]
    unnamed x13 -> x1, local copies, waits for them, and re-layouts: 7.71 us -> 2.02 us
where the time goes in v1:
time: 45 us; the launch traced here: 44.9 us
  Pallas kernels  42.9 us (95%)
  local copies, waits for them, and re-layouts  2.02 us (4%)
    pallas_call x1, Pallas kernels, local_steps(): pl.pallas_call(functools.partial(adi_kernel, (('row', parts_x), ('col', p...  42.9 us
    unnamed x1, local copies, waits for them, and re-layouts  2.02 us

profile of v1, /device:TPU:97, one launch (start us, length us, event | category | flops | bytes accessed | tf_op | source)
XLA Modules:
  0.0 44.9 jit_solution(792618474934904062)
XLA Ops:
  0.0 42.9 %adi_steps.1 = f32[256,16,256]{2,1,0:T(8,128)S(1)} custom-call(f32[256,16,256]{2,1,0:T(8,128)} %bitcast.3, f32[256,256]{1,0:T(8,128)} %lower_x.1, f32[256,256]{1,0:T(8,128)} %diag_x.1, f32[256,256]{1,0:T(8,128)} %upper_x.1, f32[256,256]{1,0:T(8,128)} %lower_y.1, f32[256,256]{1,0:T(8,128)} %diag_y.1, f32[256,256]{1,0:T(8,128)} %upper_y.1), custom_call_target="tpu_custom_call" | custom-call | tf_op jit(solution)/shard_map/adi_steps/pallas_call | solution.py:430
  42.9 2.0 %copy.9 = f32[256,256,16]{1,2,0:T(8,128)} copy(f32[256,256,16]{1,2,0:T(8,128)S(1)} %bitcast.2) | data formatting | bytes 8388608

commit v2 on v1

--- a/solution.py
+++ b/solution.py
@@ -18,14 +18,15 @@
 
 def adi_kernel(axes, field, lower_x, diag_x, upper_x, lower_y, diag_y, upper_y, out,
                nat, stage_in, rs, hs, qs, pa, pb, pc, nd, md, ne, me_, ln, cn, un, an, m2, d2, w2, v2, r0, rn,
-               gs, gc_x, gc_y, red_x, red_y, sx, sy, ex, ey, gt, ss, halo_s, halo_r,
-               coef_sem, field_sem, gsend, grecv, send_sem, recv_sem, hsend, hrecv):
+               gs, gc_x, gc_y, red_x, red_y, sx, sy, ex, ey, raw, gt, ss, part, halo_s, halo_r,
+               coef_sem, field_sem, gsend, grecv, send_sem, recv_sem, raw_sem, hsend, hrecv):
     (row_name, parts_x), (col_name, parts_y) = axes
     n = lower_x.shape[0]
     tiles = n // LANES
     chunks = field.shape[1] // SUB
     pitch = 2 * tiles
     half = n // 2
+    group = 2
     pos = (lax.axis_index(row_name), lax.axis_index(col_name))
     parts = (parts_x, parts_y)
     names = (row_name, col_name)
@@ -35,20 +36,106 @@
     reduced = (red_x, red_y)
 
     def others(axis):
-        return [lax.rem(pos[axis] + off, parts[axis]) for off in range(1, parts[axis])]
-
+        count = parts[axis]
+        offs = sorted(range(1, count), key=lambda off: -min(off, count - off))
+        return [lax.rem(pos[axis] + off, count) for off in offs]
+
+    def field_piece(c, t):
+        return pltpu.make_async_copy(field.at[:, pl.ds(c * SUB, SUB), pl.ds(t * LANES, LANES)],
+                                     stage_in.at[c, t].reshape(n, SUB, LANES), field_sem.at[c, t])
+
+    for c in range(chunks):
+        for t in range(tiles):
+            field_piece(c, t).start()
     for slot, ref in enumerate((lower_x, diag_x, upper_x, lower_y, diag_y, upper_y)):
         pltpu.make_async_copy(ref, nat.at[slot], coef_sem).start()
-    for c in range(chunks):
-        for t in range(tiles):
-            pltpu.make_async_copy(field.at[:, pl.ds(c * SUB, SUB), pl.ds(t * LANES, LANES)],
-                                  stage_in.at[c, t].reshape(n, SUB, LANES), field_sem).start()
 
     halo_r[...] = jnp.zeros_like(halo_r)
     barrier = pltpu.get_barrier_semaphore()
     for axis in (X, Y):
         for other in others(axis):
             pl.semaphore_signal(barrier, 1, device_id={names[axis]: other}, device_id_type=MESH)
+
+    blank = jnp.zeros((SUB, LANES), F32)
+    every = tuple(range(tiles))
+    cells = [(c, t) for c in range(chunks) for t in range(tiles)]
+
+    def slab(k):
+        return pl.ds((k + 1) * PITCH, SUB)
+
+    def each_chunk(body):
+        lax.fori_loop(0, chunks, lambda c, carry: (body(c), carry)[1], 0)
+
+    def turn(src, dst, c, axis, to, kts, lts, ends, step_in=PITCH, correct=True, explicit=False, scale=None,
+             before=False, after=False):
+        def column(g, carry):
+            fs = [g * group + u for u in range(group)]
+            for kt in kts:
+                heads, tails = [None] * group, [None] * group
+                for lt in lts:
+                    if correct:
+                        rows = pl.ds(kt * (LANES * pitch) + (axis * tiles + lt), LANES, stride=pitch)
+                        near, far = w2[rows, :], v2[rows, :]
+                    if explicit:
+                        rows = pl.ds(kt * (LANES * pitch) + (axis * tiles + lt), LANES, stride=pitch)
+                        own, low, high = 2.0 - pb[rows, :], pa[rows, :], pc[rows, :]
+                    if ends:
+                        rows = pl.ds(lt * LANES * pitch + to * tiles + kt, LANES, stride=pitch)
+                        first_row, last_row = r0[rows, :], rn[rows, :]
+                    for u, f in enumerate(fs):
+                        origin = kt * LANES * step_in + (step_in if step_in == PITCH else 0) + f
+                        block = src[c, lt, pl.ds(origin, LANES, stride=step_in), :]
+                        if explicit:
+                            block = own * block - (low * src[c, lt, pl.ds(origin - step_in, LANES, stride=step_in), :]
+                                                   + high * src[c, lt, pl.ds(origin + step_in, LANES, stride=step_in), :])
+                        if correct:
+                            block = block + near * ss[0, lt, pl.ds(f, 1), :] + far * ss[1, lt, pl.ds(f, 1), :]
+                        if scale is not None:
+                            block = block * scale
+                        flipped = block.T
+                        dst[c, kt, pl.ds((lt * LANES + 1) * PITCH + f, LANES, stride=PITCH), :] = flipped
+                        if ends:
+                            fold = lambda v: v.reshape(LANES // SUB, SUB, LANES).sum(axis=0)
+                            h, s = fold(flipped * first_row), fold(flipped * last_row)
+                            heads[u] = h if heads[u] is None else heads[u] + h
+                            tails[u] = s if tails[u] is None else tails[u] + s
+                if ends:
+                    for u, f in enumerate(fs):
+                        if before:
+                            heads[u], tails[u] = heads[u] + part[0, kt, f], tails[u] + part[1, kt, f]
+                        if after:
+                            part[0, kt, f], part[1, kt, f] = heads[u], tails[u]
+                        else:
+                            ends[0][kt, pl.ds(f, 1), :] = jnp.sum(heads[u], axis=0, keepdims=True)
+                            ends[1][kt, pl.ds(f, 1), :] = jnp.sum(tails[u], axis=0, keepdims=True)
+            return carry
+
+        lax.fori_loop(0, SUB // group, column, 0, unroll=True)
+
+    for c in range(chunks):
+        for t in range(tiles):
+            field_piece(c, t).wait()
+            turn(stage_in, qs, c, X, Y, every, (t,), None, step_in=SUB, correct=False)
+    me_y = pos[Y]
+    for c, t in cells:
+        halo_s[0, c, t] = qs[c, t, slab(0), :]
+        halo_s[1, c, t] = qs[c, t, slab(n - 1), :]
+
+    def halo(side, other):
+        return pltpu.make_async_remote_copy(
+            src_ref=halo_s.at[side], dst_ref=halo_r.at[1 - side], send_sem=hsend.at[side], recv_sem=hrecv.at[1 - side],
+            device_id={col_name: other}, device_id_type=MESH)
+
+    has_before, has_after = me_y > 0, me_y < parts_y - 1
+    pl.semaphore_wait(barrier, parts_x + parts_y - 2)
+
+    @pl.when(has_before)
+    def _():
+        halo(0, me_y - 1).start()
+
+    @pl.when(has_after)
+    def _():
+        halo(1, me_y + 1).start()
 
     pltpu.make_async_copy(nat, nat, coef_sem).wait()
     for t in range(tiles):
@@ -113,7 +200,6 @@
             next_d = turned
         return prev_m, next_d
 
-    blank = jnp.zeros((SUB, LANES), F32)
     lax.fori_loop(0, blocks // step_rows, ratios, (blank, blank))
 
     first, last = pl.ds(0, pitch), pl.ds((n - 1) * pitch, pitch)
@@ -140,7 +226,6 @@
 
     for q, (ref, rows) in enumerate(((w2, first), (w2, last), (v2, first), (v2, last))):
         gs[pl.ds(q * pitch, pitch), :] = -0.5 * ref[rows, :]
-    pl.semaphore_wait(barrier, parts_x + parts_y - 2)
     for axis in (X, Y):
         gather[axis][pos[axis]] = gs[...]
         for other in others(axis):
@@ -192,67 +277,64 @@
         put(2 * count + 1, -k22 * sigma_a)
         put(2 * count + 2, mu_me)
         put(2 * count + 3, nu_me)
-
-    def publish(axis, stage, c):
+        if axis == X:
+            for p in range(count):
+                put(2 * count + 4 + p, jnp.where(p < me, mu[p], unit))
+                put(3 * count + 4 + p, jnp.where(p < me, unit, jnp.where(p > me, nu[p], nil)))
+
+    def publish(axis, stage, c, ts):
         count, table, way = parts[axis], reduced[axis], lax.rem(stage, 2)
-        for t in range(tiles):
-            head, tail = exch[axis][way, c, pos[axis], t], gt[c, t]
+        for t in ts:
+            head, tail = exch[axis][way, c, t, pos[axis]], gt[c, t]
             mu = table[pl.ds((2 * count + 2) * tiles + t, 1), :]
             nu = table[pl.ds((2 * count + 3) * tiles + t, 1), :]
             send[axis][c, 1, t] = tail + mu * head
             send[axis][c, 0, t] = head + nu * tail
+        some = pl.ds(ts[0], len(ts))
         for other in others(axis):
             sel = jnp.where(other > pos[axis], 1, 0)
             pltpu.make_async_remote_copy(
-                src_ref=send[axis].at[c, sel], dst_ref=exch[axis].at[way, c, pos[axis]],
-                send_sem=send_sem.at[axis, c], recv_sem=recv_sem.at[axis, way, c],
+                src_ref=send[axis].at[c, sel, some], dst_ref=exch[axis].at[way, c, some, pos[axis]],
+                send_sem=send_sem.at[axis, c, ts[0]], recv_sem=recv_sem.at[axis, way, c, ts[0]],
                 device_id={names[axis]: other}, device_id_type=MESH).start()
 
-    def neighbours(axis, stage, c):
+    def combine(axis, stage, c, ts):
         count, table, way = parts[axis], reduced[axis], lax.rem(stage, 2)
-        arrived = exch[axis].at[way, c, pl.ds(0, count - 1)]
-        pltpu.make_async_copy(arrived, arrived, recv_sem.at[axis, way, c]).wait()
-        pltpu.make_async_copy(arrived, arrived, send_sem.at[axis, c]).wait()
-        for t in range(tiles):
+        for t in ts:
             for side in range(2):
                 base = side * (count + 1) * tiles + t
                 total = table[pl.ds(base + count * tiles, 1), :] * gt[c, t]
                 for p in range(count):
-                    total = total + table[pl.ds(base + p * tiles, 1), :] * exch[axis][way, c, p, t]
+                    total = total + table[pl.ds(base + p * tiles, 1), :] * exch[axis][way, c, t, p]
                 ss[side, t] = total
 
-    def turn(src, dst, c, axis, to, stage, correct, dots, step_in=PITCH):
+    def neighbours(axis, stage, c, ts):
         way = lax.rem(stage, 2)
-
-        def column(f, kt):
-            heads = tails = None
-            for lt in range(tiles):
-                block = src[c, lt, pl.ds(kt * (LANES * step_in) + f, LANES, stride=step_in), :]
-                if correct:
-                    rows = pl.ds(kt * (LANES * pitch) + (axis * tiles + lt), LANES, stride=pitch)
-                    block = (block + w2[rows, :] * ss[0, lt, pl.ds(f, 1), :]
-                             + v2[rows, :] * ss[1, lt, pl.ds(f, 1), :])
-                if dots is None:
-                    block = block * 0.5
-                flipped = block.T
-                dst[c, kt, pl.ds(lt * LANES * PITCH + f, LANES, stride=PITCH), :] = flipped
-                if dots:
-                    rows = pl.ds(lt * LANES * pitch + to * tiles + kt, LANES, stride=pitch)
-                    fold = lambda v: v.reshape(LANES // SUB, SUB, LANES).sum(axis=0)
-                    h, s = fold(flipped * r0[rows, :]), fold(flipped * rn[rows, :])
-                    heads = h if heads is None else heads + h
-                    tails = s if tails is None else tails + s
-            if dots:
-                exch[to][way, c, pos[to], kt, pl.ds(f, 1), :] = jnp.sum(heads, axis=0, keepdims=True)
-                gt[c, kt, pl.ds(f, 1), :] = jnp.sum(tails, axis=0, keepdims=True)
-            return kt
-
-        lax.fori_loop(0, tiles, lambda kt, carry: (lax.fori_loop(0, SUB, column, kt, unroll=True), carry)[1], 0)
-
-    cells = [(c, t) for c in range(chunks) for t in range(tiles)]
-
-    def slab(k):
-        return pl.ds(k * PITCH, SUB)
+        arrived = exch[axis].at[way, c, pl.ds(ts[0], len(ts)), pl.ds(0, parts[axis] - 1)]
+        pltpu.make_async_copy(arrived, arrived, recv_sem.at[axis, way, c, ts[0]]).wait()
+        pltpu.make_async_copy(arrived, arrived, send_sem.at[axis, c, ts[0]]).wait()
+        combine(axis, stage, c, ts)
+
+    def publish_raw(c):
+        for t in range(tiles):
+            raw[c, pos[X], 0, t] = exch[X][0, c, t, pos[X]]
+            raw[c, pos[X], 1, t] = gt[c, t]
+        for other in others(X):
+            pltpu.make_async_remote_copy(
+                src_ref=raw.at[c, pos[X]], dst_ref=raw.at[c, pos[X]], send_sem=raw_sem.at[0, c], recv_sem=raw_sem.at[1, c],
+                device_id={row_name: other}, device_id_type=MESH).start()
+
+    def neighbours_raw(c):
+        count = parts_x
+        arrived = raw.at[c, pl.ds(0, count - 1)]
+        pltpu.make_async_copy(arrived, arrived, raw_sem.at[1, c]).wait()
+        pltpu.make_async_copy(arrived, arrived, raw_sem.at[0, c]).wait()
+        for t in range(tiles):
+            for p in range(count):
+                on_head = red_x[pl.ds((2 * count + 4 + p) * tiles + t, 1), :]
+                on_tail = red_x[pl.ds((3 * count + 4 + p) * tiles + t, 1), :]
+                exch[X][0, c, t, p] = on_head * raw[c, p, 0, t] + on_tail * raw[c, p, 1, t]
+        combine(X, 0, c, every)
 
     def solve_block(axis, minus):
         def coef(array, k, t):
@@ -261,11 +343,14 @@
         def forward(k, state):
             ups, downs = list(state[0]), list(state[1])
             r = n - 1 - k
-            for s, (c, t) in enumerate(cells):
-                ups[s] = rs[c, t, slab(k), :] + coef(ln, k, t) * ups[s]
-                hs[c, t, slab(k), :] = ups[s]
-                downs[s] = rs[c, t, slab(r), :] + coef(un, r, t) * downs[s]
-                hs[c, t, slab(r), :] = downs[s]
+            for t in range(tiles):
+                up, down = coef(ln, k, t), coef(un, r, t)
+                for c in range(chunks):
+                    s = c * tiles + t
+                    ups[s] = rs[c, t, slab(k), :] + up * ups[s]
+                    hs[c, t, slab(k), :] = ups[s]
+                    downs[s] = rs[c, t, slab(r), :] + down * downs[s]
+                    hs[c, t, slab(r), :] = downs[s]
             return tuple(ups), tuple(downs)
 
         init = tuple(blank for _ in cells)
@@ -289,11 +374,14 @@
         def backward(step, state):
             lows, highs = list(state[0]), list(state[1])
             k, r = half - 1 - step, half + step
-            for s, (c, t) in enumerate(cells):
-                lows[s] = coef(m2, k, t) * hs[c, t, slab(k), :] + coef(cn, k, t) * lows[s]
-                place(c, t, k, lows[s])
-                highs[s] = coef(d2, r, t) * hs[c, t, slab(r), :] + coef(an, r, t) * highs[s]
-                place(c, t, r, highs[s])
+            for t in range(tiles):
+                m_low, c_low, m_high, a_high = coef(m2, k, t), coef(cn, k, t), coef(d2, r, t), coef(an, r, t)
+                for c in range(chunks):
+                    s = c * tiles + t
+                    lows[s] = m_low * hs[c, t, slab(k), :] + c_low * lows[s]
+                    place(c, t, k, lows[s])
+                    highs[s] = m_high * hs[c, t, slab(r), :] + a_high * highs[s]
+                    place(c, t, r, highs[s])
             return tuple(lows), tuple(highs)
 
         state = lax.fori_loop(1, unroll, backward, (tuple(low_s), tuple(high_s)), unroll=True)
@@ -301,41 +389,6 @@
 
     def each_chunk(body):
         lax.fori_loop(0, chunks, lambda c, carry: (body(c), carry)[1], 0)
-
-    pltpu.make_async_copy(stage_in, stage_in, field_sem).wait()
-    each_chunk(lambda c: turn(stage_in, rs, c, X, Y, 0, False, False, SUB))
-    me_y = pos[Y]
-    for c, t in cells:
-        halo_s[0, c, t] = rs[c, t, slab(0), :]
-        halo_s[1, c, t] = rs[c, t, slab(n - 1), :]
-
-    def halo(side, other):
-        return pltpu.make_async_remote_copy(
-            src_ref=halo_s.at[side], dst_ref=halo_r.at[1 - side], send_sem=hsend.at[side], recv_sem=hrecv.at[1 - side],
-            device_id={col_name: other}, device_id_type=MESH)
-
-    has_before, has_after = me_y > 0, me_y < parts_y - 1
-
-    @pl.when(has_before)
-    def _():
-        halo(0, me_y - 1).start()
-
-    @pl.when(has_after)
-    def _():
-        halo(1, me_y + 1).start()
-
-    def explicit(k, state):
-        befores, heres = list(state[0]), list(state[1])
-        coef = lambda array, t: array[pl.ds(k * pitch + tiles + t, 1), :]
-        for s, (c, t) in enumerate(cells):
-            ahead = rs[c, t, slab(k + 1), :]
-            qs[c, t, slab(k), :] = (2.0 - coef(pb, t)) * heres[s] - (coef(pa, t) * befores[s] + coef(pc, t) * ahead)
-            befores[s], heres[s] = heres[s], ahead
-        return tuple(befores), tuple(heres)
-
-    befores, heres = lax.fori_loop(
-        0, n - unroll, explicit, (tuple(blank for _ in cells), tuple(rs[c, t, slab(0), :] for c, t in cells)), unroll=unroll)
-    befores, heres = lax.fori_loop(n - unroll, n - 1, explicit, (befores, heres), unroll=True)
 
     @pl.when(has_before)
     def _():
@@ -347,50 +400,62 @@
         halo(1, me_y + 1).wait_send()
         halo(0, me_y + 1).wait_recv()
 
-    for s, (c, t) in enumerate(cells):
-        here = pl.ds((n - 1) * pitch + tiles + t, 1)
-        qs[c, t, slab(n - 1), :] = (2.0 - pb[here, :]) * heres[s] - (pa[here, :] * befores[s] + pc[here, :] * halo_r[1, c, t])
-        qs[c, t, slab(0), :] = qs[c, t, slab(0), :] - pa[pl.ds(tiles + t, 1), :] * halo_r[0, c, t]
+    for c, t in cells:
+        qs[c, t, slab(-1), :] = halo_r[0, c, t]
+        qs[c, t, slab(n), :] = halo_r[1, c, t]
+
+    def ends_of(axis, stage, c):
+        at = exch[axis].at[lax.rem(stage, 2), c, :, pos[axis]]
+        return at, gt.at[c]
 
     def start_x(c):
-        turn(qs, rs, c, Y, X, 0, False, True)
-        publish(X, 0, c)
-
+        turn(qs, rs, c, Y, X, every, every, ends_of(X, 0, c), correct=False, explicit=True)
+        publish_raw(c)
+
+    def to_y(stage, c):
+        for kt in every:
+            turn(qs, rs, c, X, Y, (kt,), every, ends_of(Y, stage, c))
+            publish(Y, stage, c, (kt,))
+
+    def to_x(stage, c):
+        for lt in every:
+            neighbours(Y, stage, c, (lt,))
+            turn(qs, rs, c, Y, X, every, (lt,), ends_of(X, stage + 1, c), before=lt > 0, after=lt < tiles - 1)
+        publish(X, stage + 1, c, every)
+
+    each_chunk(start_x)
+    solve_block(X, True)
     reduce_lines(X)
-    each_chunk(start_x)
     reduce_lines(Y)
     sent = gc_x.at[pl.ds(0, parts_x - 1)]
     pltpu.make_async_copy(sent, sent, gsend).wait()
     sent = gc_y.at[pl.ds(0, parts_y - 1)]
     pltpu.make_async_copy(sent, sent, gsend).wait()
 
-    def x_half(stage):
-        def finish(c):
-            neighbours(X, stage, c)
-            turn(qs, rs, c, X, Y, stage, True, True)
-            publish(Y, stage, c)
-
+    def first_to_y(c):
+        neighbours_raw(c)
+        to_y(0, c)
+
+    each_chunk(first_to_y)
+
+    def step(stage, carry):
+        def onward(c):
+            neighbours(X, stage, c, every)
+            to_y(stage, c)
+
+        solve_block(Y, True)
+        each_chunk(lambda c: to_x(stage - 1, c))
         solve_block(X, True)
-        each_chunk(finish)
-
-    def step(stage, carry):
-        def finish(c):
-            neighbours(Y, stage, c)
-            turn(qs, rs, c, Y, X, stage + 1, True, True)
-            publish(X, stage + 1, c)
-
-        x_half(stage)
-        solve_block(Y, True)
-        each_chunk(finish)
+        each_chunk(onward)
         return carry
 
-    lax.fori_loop(0, STEPS - 1, step, 0)
-    x_half(STEPS - 1)
+    lax.fori_loop(1, STEPS, step, 0)
     solve_block(Y, False)
 
     def finish(c):
-        neighbours(Y, STEPS - 1, c)
-        turn(qs, rs, c, Y, X, STEPS, True, None)
+        for lt in every:
+            neighbours(Y, STEPS - 1, c, (lt,))
+            turn(qs, rs, c, Y, X, every, (lt,), None, scale=0.5)
 
         def unload(k, carry):
             for t in range(tiles):
@@ -411,19 +476,22 @@
         n, fields = field.shape[0], field.shape[2]
         tiles, chunks = n // LANES, fields // SUB
         packed = pltpu.VMEM((n * 2 * tiles, LANES), F32)
-        big = pltpu.VMEM((chunks, tiles, n * PITCH, LANES), F32)
+        plane = -(-((n + 2) * PITCH - SUB) // (4 * SUB)) * 4 * SUB + SUB
+        big = pltpu.VMEM((chunks, tiles, plane, LANES), F32)
         dma = pltpu.SemaphoreType.DMA
         sends = pltpu.VMEM((chunks, 2, tiles, SUB, LANES), F32)
-        line = lambda count: pltpu.VMEM((2, chunks, count, tiles, SUB, LANES), F32)
-        table = lambda count: pltpu.VMEM(((2 * count + 4) * tiles, LANES), F32)
+        line = lambda count: pltpu.VMEM((2, chunks, tiles, count, SUB, LANES), F32)
+        table = lambda count: pltpu.VMEM(((4 * count + 4) * tiles, LANES), F32)
         small = pltpu.VMEM((2, chunks, tiles, SUB, LANES), F32)
         message = (8 * tiles, LANES)
         scratch = [
             pltpu.VMEM((6, n, n), F32), pltpu.VMEM((chunks, tiles, n * SUB, LANES), F32), big, big, big, *([packed] * 17),
             pltpu.VMEM(message, F32), pltpu.VMEM((parts_x,) + message, F32), pltpu.VMEM((parts_y,) + message, F32),
             table(parts_x), table(parts_y), sends, sends, line(parts_x), line(parts_y),
-            pltpu.VMEM((chunks, tiles, SUB, LANES), F32), pltpu.VMEM((2, tiles, SUB, LANES), F32), small, small,
-            dma, dma, dma, dma((2,)), dma((2, chunks)), dma((2, 2, chunks)), dma((2,)), dma((2,)),
+            pltpu.VMEM((chunks, parts_x, 2, tiles, SUB, LANES), F32),
+            pltpu.VMEM((chunks, tiles, SUB, LANES), F32), pltpu.VMEM((2, tiles, SUB, LANES), F32),
+            pltpu.VMEM((2, tiles, SUB, SUB, LANES), F32), small, small,
+            dma, dma((chunks, tiles)), dma, dma((2,)), dma((2, chunks, tiles)), dma((2, 2, chunks, tiles)), dma((2, chunks)), dma((2,)), dma((2,)),
         ]
         in_hbm = pl.BlockSpec(memory_space=pltpu.HBM)
         turned = jnp.transpose(field, (0, 2, 1))

time: 45 us -> 40.8 us (0.907)
  Pallas kernels: 42.9 us -> 38.7 us
    pallas_call x1, Pallas kernels: 42.9 us -> 38.7 us  [local_steps(): pl.pallas_call(functools.partial(adi_kernel, (('row', parts_x), ('col', p...]
where the time goes in v2:
time: 40.8 us
  Pallas kernels  38.7 us (95%)
  local copies, waits for them, and re-layouts  2.02 us (5%)
    pallas_call x1, Pallas kernels, local_steps(): pl.pallas_call(functools.partial(adi_kernel, (('row', parts_x), ('col', p...  38.7 us
    unnamed x1, local copies, waits for them, and re-layouts  2.02 us

profile of v2, /device:TPU:97, one launch (start us, length us, event | category | flops | bytes accessed | tf_op | source)
XLA Modules:
  0.0 40.8 jit_solution(4938575341017938957)
XLA Ops:
  0.0 38.7 %adi_steps.1 = f32[256,16,256]{2,1,0:T(8,128)S(1)} custom-call(f32[256,16,256]{2,1,0:T(8,128)} %bitcast.3, f32[256,256]{1,0:T(8,128)} %lower_x.1, f32[256,256]{1,0:T(8,128)} %diag_x.1, f32[256,256]{1,0:T(8,128)} %upper_x.1, f32[256,256]{1,0:T(8,128)} %lower_y.1, f32[256,256]{1,0:T(8,128)} %diag_y.1, f32[256,256]{1,0:T(8,128)} %upper_y.1), custom_call_target="tpu_custom_call" | custom-call | tf_op jit(solution)/shard_map/adi_steps/pallas_call | solution.py:498
  38.8 2.0 %copy.9 = f32[256,256,16]{1,2,0:T(8,128)} copy(f32[256,256,16]{1,2,0:T(8,128)S(1)} %bitcast.2) | data formatting | bytes 8388608

commit v3 on v2

--- a/solution.py
+++ b/solution.py
@@ -12,12 +12,12 @@
 LANES = 128
 SUB = 8
 PITCH = SUB + 1
-MESH = pl.DeviceIdType.MESH
+LOGICAL = pl.DeviceIdType.LOGICAL
 X, Y = 0, 1
 
 
-def adi_kernel(axes, field, lower_x, diag_x, upper_x, lower_y, diag_y, upper_y, out,
-               nat, stage_in, rs, hs, qs, pa, pb, pc, nd, md, ne, me_, ln, cn, un, an, m2, d2, w2, v2, r0, rn,
+def adi_kernel(axes, strides, field, lower_x, diag_x, upper_x, lower_y, diag_y, upper_y, out,
+               nat, rs, hs, qs, pa, pb, pc, nd, md, ne, me_, ln, cn, un, an, m2, d2, w2, v2, r0, rn,
                gs, gc_x, gc_y, red_x, red_y, sx, sy, ex, ey, raw, gt, ss, part, halo_s, halo_r,
                coef_sem, field_sem, gsend, grecv, send_sem, recv_sem, raw_sem, hsend, hrecv):
     (row_name, parts_x), (col_name, parts_y) = axes
@@ -29,12 +29,15 @@
     group = 2
     pos = (lax.axis_index(row_name), lax.axis_index(col_name))
     parts = (parts_x, parts_y)
-    names = (row_name, col_name)
+    home = sum(lax.axis_index(name) * stride for name, stride in strides.items())
     exch = (ex, ey)
     send = (sx, sy)
     gather = (gc_x, gc_y)
     reduced = (red_x, red_y)
 
+    def device(axis, other):
+        return home + (other - pos[axis]) * strides[(row_name, col_name)[axis]]
+
     def others(axis):
         count = parts[axis]
         offs = sorted(range(1, count), key=lambda off: -min(off, count - off))
@@ -42,7 +45,7 @@
 
     def field_piece(c, t):
         return pltpu.make_async_copy(field.at[:, pl.ds(c * SUB, SUB), pl.ds(t * LANES, LANES)],
-                                     stage_in.at[c, t].reshape(n, SUB, LANES), field_sem.at[c, t])
+                                     out.at[c, t].reshape(n, SUB, LANES), field_sem.at[c, t])
 
     for c in range(chunks):
         for t in range(tiles):
@@ -54,7 +57,7 @@
     barrier = pltpu.get_barrier_semaphore()
     for axis in (X, Y):
         for other in others(axis):
-            pl.semaphore_signal(barrier, 1, device_id={names[axis]: other}, device_id_type=MESH)
+            pl.semaphore_signal(barrier, 1, device_id=device(axis, other), device_id_type=LOGICAL)
 
     blank = jnp.zeros((SUB, LANES), F32)
     every = tuple(range(tiles))
@@ -67,7 +70,7 @@
         lax.fori_loop(0, chunks, lambda c, carry: (body(c), carry)[1], 0)
 
     def turn(src, dst, c, axis, to, kts, lts, ends, step_in=PITCH, correct=True, explicit=False, scale=None,
-             before=False, after=False):
+             before=False, after=False, step_out=PITCH):
         def column(g, carry):
             fs = [g * group + u for u in range(group)]
             for kt in kts:
@@ -84,6 +87,7 @@
                         first_row, last_row = r0[rows, :], rn[rows, :]
                     for u, f in enumerate(fs):
                         origin = kt * LANES * step_in + (step_in if step_in == PITCH else 0) + f
+                        target = lt * LANES * step_out + (step_out if step_out == PITCH else 0) + f
                         block = src[c, lt, pl.ds(origin, LANES, stride=step_in), :]
                         if explicit:
                             block = own * block - (low * src[c, lt, pl.ds(origin - step_in, LANES, stride=step_in), :]
@@ -93,7 +97,7 @@
                         if scale is not None:
                             block = block * scale
                         flipped = block.T
-                        dst[c, kt, pl.ds((lt * LANES + 1) * PITCH + f, LANES, stride=PITCH), :] = flipped
+                        dst[c, kt, pl.ds(target, LANES, stride=step_out), :] = flipped
                         if ends:
                             fold = lambda v: v.reshape(LANES // SUB, SUB, LANES).sum(axis=0)
                             h, s = fold(flipped * first_row), fold(flipped * last_row)
@@ -115,7 +119,7 @@
     for c in range(chunks):
         for t in range(tiles):
             field_piece(c, t).wait()
-            turn(stage_in, qs, c, X, Y, every, (t,), None, step_in=SUB, correct=False)
+            turn(out, qs, c, X, Y, every, (t,), None, step_in=SUB, correct=False)
     me_y = pos[Y]
     for c, t in cells:
         halo_s[0, c, t] = qs[c, t, slab(0), :]
@@ -124,7 +128,7 @@
     def halo(side, other):
         return pltpu.make_async_remote_copy(
             src_ref=halo_s.at[side], dst_ref=halo_r.at[1 - side], send_sem=hsend.at[side], recv_sem=hrecv.at[1 - side],
-            device_id={col_name: other}, device_id_type=MESH)
+            device_id=device(Y, other), device_id_type=LOGICAL)
 
     has_before, has_after = me_y > 0, me_y < parts_y - 1
     pl.semaphore_wait(barrier, parts_x + parts_y - 2)
@@ -231,7 +235,7 @@
         for other in others(axis):
             pltpu.make_async_remote_copy(
                 src_ref=gs, dst_ref=gather[axis].at[pos[axis]], send_sem=gsend, recv_sem=grecv.at[axis],
-                device_id={names[axis]: other}, device_id_type=MESH).start()
+                device_id=device(axis, other), device_id_type=LOGICAL).start()
 
     def reduce_lines(axis):
         count, me = parts[axis], pos[axis]
@@ -282,21 +286,25 @@
                 put(2 * count + 4 + p, jnp.where(p < me, mu[p], unit))
                 put(3 * count + 4 + p, jnp.where(p < me, unit, jnp.where(p > me, nu[p], nil)))
 
+    def slot(axis, way, c, t, p):
+        return (way, c, p, t) if axis == X else (way, c, t, p)
+
     def publish(axis, stage, c, ts):
         count, table, way = parts[axis], reduced[axis], lax.rem(stage, 2)
         for t in ts:
-            head, tail = exch[axis][way, c, t, pos[axis]], gt[c, t]
+            head, tail = exch[axis][slot(axis, way, c, t, pos[axis])], gt[c, t]
             mu = table[pl.ds((2 * count + 2) * tiles + t, 1), :]
             nu = table[pl.ds((2 * count + 3) * tiles + t, 1), :]
             send[axis][c, 1, t] = tail + mu * head
             send[axis][c, 0, t] = head + nu * tail
         some = pl.ds(ts[0], len(ts))
+        there = exch[X].at[way, c, pos[X]] if axis == X else exch[Y].at[way, c, some, pos[Y]]
         for other in others(axis):
             sel = jnp.where(other > pos[axis], 1, 0)
             pltpu.make_async_remote_copy(
-                src_ref=send[axis].at[c, sel, some], dst_ref=exch[axis].at[way, c, some, pos[axis]],
+                src_ref=send[axis].at[c, sel, some], dst_ref=there,
                 send_sem=send_sem.at[axis, c, ts[0]], recv_sem=recv_sem.at[axis, way, c, ts[0]],
-                device_id={names[axis]: other}, device_id_type=MESH).start()
+                device_id=device(axis, other), device_id_type=LOGICAL).start()
 
     def combine(axis, stage, c, ts):
         count, table, way = parts[axis], reduced[axis], lax.rem(stage, 2)
@@ -305,24 +313,25 @@
                 base = side * (count + 1) * tiles + t
                 total = table[pl.ds(base + count * tiles, 1), :] * gt[c, t]
                 for p in range(count):
-                    total = total + table[pl.ds(base + p * tiles, 1), :] * exch[axis][way, c, t, p]
+                    total = total + table[pl.ds(base + p * tiles, 1), :] * exch[axis][slot(axis, way, c, t, p)]
                 ss[side, t] = total
 
     def neighbours(axis, stage, c, ts):
         way = lax.rem(stage, 2)
-        arrived = exch[axis].at[way, c, pl.ds(ts[0], len(ts)), pl.ds(0, parts[axis] - 1)]
+        some = pl.ds(0, parts[axis] - 1)
+        arrived = exch[X].at[way, c, some] if axis == X else exch[Y].at[way, c, pl.ds(ts[0], len(ts)), some]
         pltpu.make_async_copy(arrived, arrived, recv_sem.at[axis, way, c, ts[0]]).wait()
         pltpu.make_async_copy(arrived, arrived, send_sem.at[axis, c, ts[0]]).wait()
         combine(axis, stage, c, ts)
 
     def publish_raw(c):
         for t in range(tiles):
-            raw[c, pos[X], 0, t] = exch[X][0, c, t, pos[X]]
+            raw[c, pos[X], 0, t] = exch[X][slot(X, 0, c, t, pos[X])]
             raw[c, pos[X], 1, t] = gt[c, t]
         for other in others(X):
             pltpu.make_async_remote_copy(
                 src_ref=raw.at[c, pos[X]], dst_ref=raw.at[c, pos[X]], send_sem=raw_sem.at[0, c], recv_sem=raw_sem.at[1, c],
-                device_id={row_name: other}, device_id_type=MESH).start()
+                device_id=device(X, other), device_id_type=LOGICAL).start()
 
     def neighbours_raw(c):
         count = parts_x
@@ -333,7 +342,7 @@
             for p in range(count):
                 on_head = red_x[pl.ds((2 * count + 4 + p) * tiles + t, 1), :]
                 on_tail = red_x[pl.ds((3 * count + 4 + p) * tiles + t, 1), :]
-                exch[X][0, c, t, p] = on_head * raw[c, p, 0, t] + on_tail * raw[c, p, 1, t]
+                exch[X][slot(X, 0, c, t, p)] = on_head * raw[c, p, 0, t] + on_tail * raw[c, p, 1, t]
         combine(X, 0, c, every)
 
     def solve_block(axis, minus):
@@ -405,8 +414,8 @@
         qs[c, t, slab(n), :] = halo_r[1, c, t]
 
     def ends_of(axis, stage, c):
-        at = exch[axis].at[lax.rem(stage, 2), c, :, pos[axis]]
-        return at, gt.at[c]
+        way = lax.rem(stage, 2)
+        return exch[X].at[way, c, pos[X]] if axis == X else exch[Y].at[way, c, :, pos[Y]], gt.at[c]
 
     def start_x(c):
         turn(qs, rs, c, Y, X, every, every, ends_of(X, 0, c), correct=False, explicit=True)
@@ -455,20 +464,27 @@
     def finish(c):
         for lt in every:
             neighbours(Y, STEPS - 1, c, (lt,))
-            turn(qs, rs, c, Y, X, every, (lt,), None, scale=0.5)
-
-        def unload(k, carry):
-            for t in range(tiles):
-                out[k, pl.ds(pl.multiple_of(c * SUB, SUB), SUB), pl.ds(t * LANES, LANES)] = rs[c, t, slab(k), :]
-            return carry
-
-        lax.fori_loop(0, n, unload, 0, unroll=unroll)
+            turn(qs, out, c, Y, X, every, (lt,), None, scale=0.5, step_out=SUB)
 
     each_chunk(finish)
+
+
+def unload_kernel(tiles_ref, out, sem):
+    chunks, tiles, rows, lanes = tiles_ref.shape
+    copies = [pltpu.make_async_copy(tiles_ref.at[c, t].reshape(rows // SUB, SUB, lanes),
+                                    out.at[:, pl.ds(c * SUB, SUB), pl.ds(t * lanes, lanes)], sem.at[c * tiles + t])
+              for c in range(chunks) for t in range(tiles)]
+    for copy in copies:
+        copy.start()
+    for copy in copies:
+        copy.wait()
 
 
 def solution(mesh):
     parts_x, parts_y = mesh.shape["row"], mesh.shape["col"]
+    strides, stride = {}, 1
+    for name in reversed(mesh.axis_names):
+        strides[name], stride = stride, stride * mesh.shape[name]
     field_spec = P(("batch", "row"), "col", None)
     coeff_spec = P(("batch", "row"), "col")
 
@@ -480,14 +496,13 @@
         big = pltpu.VMEM((chunks, tiles, plane, LANES), F32)
         dma = pltpu.SemaphoreType.DMA
         sends = pltpu.VMEM((chunks, 2, tiles, SUB, LANES), F32)
-        line = lambda count: pltpu.VMEM((2, chunks, tiles, count, SUB, LANES), F32)
         table = lambda count: pltpu.VMEM(((4 * count + 4) * tiles, LANES), F32)
         small = pltpu.VMEM((2, chunks, tiles, SUB, LANES), F32)
         message = (8 * tiles, LANES)
         scratch = [
-            pltpu.VMEM((6, n, n), F32), pltpu.VMEM((chunks, tiles, n * SUB, LANES), F32), big, big, big, *([packed] * 17),
+            pltpu.VMEM((6, n, n), F32), big, big, big, *([packed] * 17),
             pltpu.VMEM(message, F32), pltpu.VMEM((parts_x,) + message, F32), pltpu.VMEM((parts_y,) + message, F32),
-            table(parts_x), table(parts_y), sends, sends, line(parts_x), line(parts_y),
+            table(parts_x), table(parts_y), sends, sends, pltpu.VMEM((2, chunks, parts_x, tiles, SUB, LANES), F32), pltpu.VMEM((2, chunks, tiles, parts_y, SUB, LANES), F32),
             pltpu.VMEM((chunks, parts_x, 2, tiles, SUB, LANES), F32),
             pltpu.VMEM((chunks, tiles, SUB, LANES), F32), pltpu.VMEM((2, tiles, SUB, LANES), F32),
             pltpu.VMEM((2, tiles, SUB, SUB, LANES), F32), small, small,
@@ -495,13 +510,19 @@
         ]
         in_hbm = pl.BlockSpec(memory_space=pltpu.HBM)
         turned = jnp.transpose(field, (0, 2, 1))
+        in_vmem = pl.BlockSpec(memory_space=pltpu.VMEM)
+        tiled = pl.pallas_call(
+            functools.partial(adi_kernel, (("row", parts_x), ("col", parts_y)), strides),
+            out_shape=jax.ShapeDtypeStruct((chunks, tiles, n * SUB, LANES), F32),
+            in_specs=[in_hbm] * 7, out_specs=in_vmem, scratch_shapes=scratch,
+            compiler_params=pltpu.CompilerParams(collective_id=0, has_side_effects=True, vmem_limit_bytes=40 * 1024 * 1024),
+            name="adi_steps",
+        )(*(pltpu.with_memory_space_constraint(array, pltpu.HBM) for array in (turned,) + coeffs))
         result = pl.pallas_call(
-            functools.partial(adi_kernel, (("row", parts_x), ("col", parts_y))),
-            out_shape=jax.ShapeDtypeStruct(turned.shape, F32),
-            in_specs=[in_hbm] * 7, out_specs=pl.BlockSpec(memory_space=pltpu.VMEM), scratch_shapes=scratch,
-            compiler_params=pltpu.CompilerParams(collective_id=0, has_side_effects=True, vmem_limit_bytes=48 * 1024 * 1024),
-            name="adi_steps",
-        )(turned, *(pltpu.with_memory_space_constraint(array, pltpu.HBM) for array in coeffs))
+            unload_kernel, out_shape=jax.ShapeDtypeStruct(turned.shape, F32), in_specs=[in_vmem], out_specs=in_hbm,
+            scratch_shapes=[dma((chunks * tiles,))], compiler_params=pltpu.CompilerParams(vmem_limit_bytes=1024 * 1024),
+            name="unload",
+        )(tiled)
         return jnp.transpose(result, (0, 2, 1))
 
     return jax.shard_map(local_steps, mesh=mesh, in_specs=(field_spec,) + (coeff_spec,) * 6, out_specs=field_spec, check_vma=False)

time: 40.8 us -> 39.9 us (0.978)
  local copies, waits for them, and re-layouts: 2.02 us -> 0 us
  Pallas kernels: 38.7 us -> 39.8 us
    pallas_call x0 -> x1, Pallas kernels: none -> 2.04 us  [local_steps(): pl.pallas_call(unload_kernel, out_shape=jax.ShapeDtypeStruct(turned.shape...]
    unnamed x1 -> x0, local copies, waits for them, and re-layouts: 2.02 us -> none
    pallas_call x1, Pallas kernels: 38.7 us -> 37.8 us  [local_steps(): pl.pallas_call(functools.partial(adi_kernel, (('row', parts_x), ('col', p...]
where the time goes in v3:
time: 39.9 us; the launch traced here: 39.8 us
  Pallas kernels  39.8 us (100%)
    pallas_call x1, Pallas kernels, local_steps(): pl.pallas_call(functools.partial(adi_kernel, (('row', parts_x), ('col', p...  37.8 us
    pallas_call x1, Pallas kernels, local_steps(): pl.pallas_call(unload_kernel, out_shape=jax.ShapeDtypeStruct(turned.shape...  2.04 us

profile of v3, /device:TPU:97, one launch (start us, length us, event | category | flops | bytes accessed | tf_op | source)
XLA Modules:
  0.0 39.8 jit_solution(14203375519108593351)
XLA Ops:
  0.0 37.8 %adi_steps.1.tiles_ref = f32[2,2,2048,128]{3,2,1,0:T(8,128)S(1)} custom-call(f32[256,16,256]{2,1,0:T(8,128)} %bitcast.2, f32[256,256]{1,0:T(8,128)} %lower_x.1, f32[256,256]{1,0:T(8,128)} %diag_x.1, f32[256,256]{1,0:T(8,128)} %upper_x.1, f32[256,256]{1,0:T(8,128)} %lower_y.1, f32[256,256]{1,0:T(8,128)} %diag_y.1, f32[256,256]{1,0:T(8,128)} %upper_y.1), custom_call_target="tpu_custom_call" | custom-call | tf_op jit(solution)/shard_map/adi_steps/pallas_call | solution.py:514
  37.8 2.0 %unload.1 = f32[256,16,256]{2,1,0:T(8,128)} custom-call(f32[2,2,2048,128]{3,2,1,0:T(8,128)S(1)} %adi_steps.1.tiles_ref), custom_call_target="tpu_custom_call" | custom-call | tf_op jit(solution)/shard_map/unload/pallas_call | solution.py:521

commit v4 on v3

--- a/solution.py
+++ b/solution.py
@@ -16,10 +16,10 @@
 X, Y = 0, 1
 
 
-def adi_kernel(axes, strides, field, lower_x, diag_x, upper_x, lower_y, diag_y, upper_y, out,
-               nat, rs, hs, qs, pa, pb, pc, nd, md, ne, me_, ln, cn, un, an, m2, d2, w2, v2, r0, rn,
-               gs, gc_x, gc_y, red_x, red_y, sx, sy, ex, ey, raw, gt, ss, part, halo_s, halo_r,
-               coef_sem, field_sem, gsend, grecv, send_sem, recv_sem, raw_sem, hsend, hrecv):
+def adi_kernel(axes, strides, field, lower_x, diag_x, upper_x, lower_y, diag_y, upper_y, out, qs, w2, v2, ss,
+               nat, rs, hs, pa, pb, pc, nd, md, ne, me_, ln, cn, un, an, m2, d2, r0, rn,
+               gs, gc_x, gc_y, red_x, red_y, sx, sy, ex, ey, raw, gt, part, halo_s, halo_r,
+               load_sem, send_sem, recv_x, recv_y, grecv):
     (row_name, parts_x), (col_name, parts_y) = axes
     n = lower_x.shape[0]
     tiles = n // LANES
@@ -45,13 +45,13 @@
 
     def field_piece(c, t):
         return pltpu.make_async_copy(field.at[:, pl.ds(c * SUB, SUB), pl.ds(t * LANES, LANES)],
-                                     out.at[c, t].reshape(n, SUB, LANES), field_sem.at[c, t])
+                                     out.at[c, t].reshape(n, SUB, LANES), send_sem.at[t, c])
 
     for c in range(chunks):
         for t in range(tiles):
             field_piece(c, t).start()
     for slot, ref in enumerate((lower_x, diag_x, upper_x, lower_y, diag_y, upper_y)):
-        pltpu.make_async_copy(ref, nat.at[slot], coef_sem).start()
+        pltpu.make_async_copy(ref, nat.at[slot], load_sem).start()
 
     halo_r[...] = jnp.zeros_like(halo_r)
     barrier = pltpu.get_barrier_semaphore()
@@ -116,32 +116,50 @@
 
         lax.fori_loop(0, SUB // group, column, 0, unroll=True)
 
+    me_y = pos[Y]
+    has_before, has_after = me_y > 0, me_y < parts_y - 1
+
+    def halo(side, c, other):
+        return pltpu.make_async_remote_copy(
+            src_ref=halo_s.at[side, c], dst_ref=halo_r.at[1 - side, c], send_sem=send_sem.at[side, c], recv_sem=recv_y.at[1, c, 1 - side],
+            device_id=device(Y, other), device_id_type=LOGICAL)
+
+    def send_halo(c):
+        for t in every:
+            halo_s[0, c, t] = qs[c, t, slab(0), :]
+            halo_s[1, c, t] = qs[c, t, slab(n - 1), :]
+
+        @pl.when(has_before)
+        def _():
+            halo(0, c, me_y - 1).start()
+
+        @pl.when(has_after)
+        def _():
+            halo(1, c, me_y + 1).start()
+
+    def await_halo(c):
+        @pl.when(has_before)
+        def _():
+            halo(0, c, me_y - 1).wait_send()
+            halo(1, c, me_y - 1).wait_recv()
+
+        @pl.when(has_after)
+        def _():
+            halo(1, c, me_y + 1).wait_send()
+            halo(0, c, me_y + 1).wait_recv()
+
+        for t in every:
+            qs[c, t, slab(-1), :] = halo_r[0, c, t]
+            qs[c, t, slab(n), :] = halo_r[1, c, t]
+
     for c in range(chunks):
         for t in range(tiles):
             field_piece(c, t).wait()
             turn(out, qs, c, X, Y, every, (t,), None, step_in=SUB, correct=False)
-    me_y = pos[Y]
-    for c, t in cells:
-        halo_s[0, c, t] = qs[c, t, slab(0), :]
-        halo_s[1, c, t] = qs[c, t, slab(n - 1), :]
-
-    def halo(side, other):
-        return pltpu.make_async_remote_copy(
-            src_ref=halo_s.at[side], dst_ref=halo_r.at[1 - side], send_sem=hsend.at[side], recv_sem=hrecv.at[1 - side],
-            device_id=device(Y, other), device_id_type=LOGICAL)
-
-    has_before, has_after = me_y > 0, me_y < parts_y - 1
-    pl.semaphore_wait(barrier, parts_x + parts_y - 2)
-
-    @pl.when(has_before)
-    def _():
-        halo(0, me_y - 1).start()
-
-    @pl.when(has_after)
-    def _():
-        halo(1, me_y + 1).start()
-
-    pltpu.make_async_copy(nat, nat, coef_sem).wait()
+        if c == 0:
+            pl.semaphore_wait(barrier, parts_x + parts_y - 2)
+        send_halo(c)
+    pltpu.make_async_copy(nat, nat, load_sem).wait()
     for t in range(tiles):
         cols = pl.ds(t * LANES, LANES)
         pa[pl.ds(t, n, stride=pitch), :] = nat[0, :, cols]
@@ -154,18 +172,18 @@
             pb[dest, :] = nat[4, rows, cols].T + 1.0
             pc[dest, :] = nat[5, rows, cols].T
 
-    unroll = 8
+    unroll, long = 8, 16
     zero = jnp.zeros((pitch, LANES), F32)
     one = jnp.ones((pitch, LANES), F32)
 
     def at_row(k, u):
-        return pl.ds(pl.multiple_of(k * (unroll * pitch), unroll * pitch) + u * pitch, pitch)
+        return pl.ds(pl.multiple_of(k * (long * pitch), long * pitch) + u * pitch, pitch)
 
     def pivots(g, state):
         dp, dq, c_prev, ep, eq, a_next = state
-        h = n // unroll - 1 - g
-        for u in range(unroll):
-            up, down = at_row(g, u), at_row(h, unroll - 1 - u)
+        h = n // long - 1 - g
+        for u in range(long):
+            up, down = at_row(g, u), at_row(h, long - 1 - u)
             nd[up, :] = dp
             new = pb[up, :] * dp - (pa[up, :] * c_prev) * dq
             md[up, :] = new
@@ -174,15 +192,17 @@
             new = pb[down, :] * ep - (a_next * pc[down, :]) * eq
             me_[down, :] = new
             ep, eq, a_next = new, ep, pa[down, :]
-            if u == unroll // 2 - 1:
+            if u % 8 == 3:
                 scale_d, scale_e = 1.0 / dp, 1.0 / ep
-        return dp * scale_d, dq * scale_d, c_prev, ep * scale_e, eq * scale_e, a_next
-
-    lax.fori_loop(0, n // unroll, pivots, (one, zero, zero, one, zero, zero))
+            if u % 8 == 7:
+                dp, dq, ep, eq = dp * scale_d, dq * scale_d, ep * scale_e, eq * scale_e
+        return dp, dq, c_prev, ep, eq, a_next
+
+    lax.fori_loop(0, n // long, pivots, (one, zero, zero, one, zero, zero))
 
     low_half = lax.broadcasted_iota(jnp.int32, (SUB, LANES), 0) < pitch
     blocks = n * pitch // SUB
-    step_rows = 4
+    step_rows = 8
 
     def ratios(g, state):
         prev_m, next_d = state
@@ -210,9 +230,9 @@
 
     def products(g, state):
         col0, row0, coln, rown, un_prev, ln_next = state
-        h = n // unroll - 1 - g
-        for u in range(unroll):
-            up, down = at_row(g, u), at_row(h, unroll - 1 - u)
+        h = n // long - 1 - g
+        for u in range(long):
+            up, down = at_row(g, u), at_row(h, long - 1 - u)
             start = jnp.logical_and(g == 0, u == 0) if u == 0 else None
             f0, f1 = an[up, :], un_prev
             b0, b1 = cn[down, :], ln_next
@@ -225,23 +245,23 @@
         return col0, row0, coln, rown, un_prev, ln_next
 
     d_first, m_last = 0.5 * d2[first, :], 0.5 * m2[last, :]
-    lax.fori_loop(0, n // unroll, products,
+    lax.fori_loop(0, n // long, products,
                   (-pa[first, :] * d2[first, :], d_first, -pc[last, :] * m2[last, :], m_last, one, one))
 
-    for q, (ref, rows) in enumerate(((w2, first), (w2, last), (v2, first), (v2, last))):
-        gs[pl.ds(q * pitch, pitch), :] = -0.5 * ref[rows, :]
     for axis in (X, Y):
-        gather[axis][pos[axis]] = gs[...]
+        for q, (ref, line) in enumerate(((w2, 0), (w2, n - 1), (v2, 0), (v2, n - 1))):
+            gs[axis, pl.ds(q * tiles, tiles), :] = -0.5 * ref[pl.ds(line * pitch + axis * tiles, tiles), :]
+        gather[axis][pos[axis]] = gs[axis]
         for other in others(axis):
             pltpu.make_async_remote_copy(
-                src_ref=gs, dst_ref=gather[axis].at[pos[axis]], send_sem=gsend, recv_sem=grecv.at[axis],
+                src_ref=gs.at[axis], dst_ref=gather[axis].at[pos[axis]], send_sem=load_sem, recv_sem=grecv.at[axis],
                 device_id=device(axis, other), device_id_type=LOGICAL).start()
 
     def reduce_lines(axis):
         count, me = parts[axis], pos[axis]
         arrived = gather[axis].at[pl.ds(0, count - 1)]
         pltpu.make_async_copy(arrived, arrived, grecv.at[axis]).wait()
-        part = lambda p, q: gather[axis][p, pl.ds(q * pitch + axis * tiles, tiles), :]
+        part = lambda p, q: gather[axis][p, pl.ds(q * tiles, tiles), :]
         nil = jnp.zeros((tiles, LANES), F32)
         unit = jnp.ones((tiles, LANES), F32)
         mu, rho, tau = [None] * count, [None] * count, [None] * count
@@ -289,6 +309,9 @@
     def slot(axis, way, c, t, p):
         return (way, c, p, t) if axis == X else (way, c, t, p)
 
+    def arrival(axis, way, c, t):
+        return recv_x.at[way, c] if axis == X else recv_y.at[way, c, t]
+
     def publish(axis, stage, c, ts):
         count, table, way = parts[axis], reduced[axis], lax.rem(stage, 2)
         for t in ts:
@@ -303,7 +326,7 @@
             sel = jnp.where(other > pos[axis], 1, 0)
             pltpu.make_async_remote_copy(
                 src_ref=send[axis].at[c, sel, some], dst_ref=there,
-                send_sem=send_sem.at[axis, c, ts[0]], recv_sem=recv_sem.at[axis, way, c, ts[0]],
+                send_sem=send_sem.at[axis, c], recv_sem=arrival(axis, way, c, ts[0]),
                 device_id=device(axis, other), device_id_type=LOGICAL).start()
 
     def combine(axis, stage, c, ts):
@@ -320,8 +343,10 @@
         way = lax.rem(stage, 2)
         some = pl.ds(0, parts[axis] - 1)
         arrived = exch[X].at[way, c, some] if axis == X else exch[Y].at[way, c, pl.ds(ts[0], len(ts)), some]
-        pltpu.make_async_copy(arrived, arrived, recv_sem.at[axis, way, c, ts[0]]).wait()
-        pltpu.make_async_copy(arrived, arrived, send_sem.at[axis, c, ts[0]]).wait()
+        pltpu.make_async_copy(arrived, arrived, arrival(axis, way, c, ts[0])).wait()
+        if ts[-1] == tiles - 1:
+            sent = arrived if axis == X else exch[Y].at[way, c, :, some]
+            pltpu.make_async_copy(sent, sent, send_sem.at[axis, c]).wait()
         combine(axis, stage, c, ts)
 
     def publish_raw(c):
@@ -330,14 +355,14 @@
             raw[c, pos[X], 1, t] = gt[c, t]
         for other in others(X):
             pltpu.make_async_remote_copy(
-                src_ref=raw.at[c, pos[X]], dst_ref=raw.at[c, pos[X]], send_sem=raw_sem.at[0, c], recv_sem=raw_sem.at[1, c],
+                src_ref=raw.at[c, pos[X]], dst_ref=raw.at[c, pos[X]], send_sem=send_sem.at[X, c], recv_sem=recv_x.at[0, c],
                 device_id=device(X, other), device_id_type=LOGICAL).start()
 
     def neighbours_raw(c):
         count = parts_x
         arrived = raw.at[c, pl.ds(0, count - 1)]
-        pltpu.make_async_copy(arrived, arrived, raw_sem.at[1, c]).wait()
-        pltpu.make_async_copy(arrived, arrived, raw_sem.at[0, c]).wait()
+        pltpu.make_async_copy(arrived, arrived, recv_x.at[0, c]).wait()
+        pltpu.make_async_copy(arrived, arrived, send_sem.at[X, c]).wait()
         for t in range(tiles):
             for p in range(count):
                 on_head = red_x[pl.ds((2 * count + 4 + p) * tiles + t, 1), :]
@@ -399,25 +424,12 @@
     def each_chunk(body):
         lax.fori_loop(0, chunks, lambda c, carry: (body(c), carry)[1], 0)
 
-    @pl.when(has_before)
-    def _():
-        halo(0, me_y - 1).wait_send()
-        halo(1, me_y - 1).wait_recv()
-
-    @pl.when(has_after)
-    def _():
-        halo(1, me_y + 1).wait_send()
-        halo(0, me_y + 1).wait_recv()
-
-    for c, t in cells:
-        qs[c, t, slab(-1), :] = halo_r[0, c, t]
-        qs[c, t, slab(n), :] = halo_r[1, c, t]
-
     def ends_of(axis, stage, c):
         way = lax.rem(stage, 2)
         return exch[X].at[way, c, pos[X]] if axis == X else exch[Y].at[way, c, :, pos[Y]], gt.at[c]
 
     def start_x(c):
+        await_halo(c)
         turn(qs, rs, c, Y, X, every, every, ends_of(X, 0, c), correct=False, explicit=True)
         publish_raw(c)
 
@@ -437,9 +449,9 @@
     reduce_lines(X)
     reduce_lines(Y)
     sent = gc_x.at[pl.ds(0, parts_x - 1)]
-    pltpu.make_async_copy(sent, sent, gsend).wait()
+    pltpu.make_async_copy(sent, sent, load_sem).wait()
     sent = gc_y.at[pl.ds(0, parts_y - 1)]
-    pltpu.make_async_copy(sent, sent, gsend).wait()
+    pltpu.make_async_copy(sent, sent, load_sem).wait()
 
     def first_to_y(c):
         neighbours_raw(c)
@@ -466,17 +478,42 @@
             neighbours(Y, STEPS - 1, c, (lt,))
             turn(qs, out, c, Y, X, every, (lt,), None, scale=0.5, step_out=SUB)
 
-    each_chunk(finish)
-
-
-def unload_kernel(tiles_ref, out, sem):
-    chunks, tiles, rows, lanes = tiles_ref.shape
-    copies = [pltpu.make_async_copy(tiles_ref.at[c, t].reshape(rows // SUB, SUB, lanes),
-                                    out.at[:, pl.ds(c * SUB, SUB), pl.ds(t * lanes, lanes)], sem.at[c * tiles + t])
-              for c in range(chunks) for t in range(tiles)]
+    lax.fori_loop(0, chunks - 1, lambda c, carry: (finish(c), carry)[1], 0)
+    for lt in every:
+        neighbours(Y, STEPS - 1, chunks - 1, (lt,))
+        if lt < tiles - 1:
+            turn(qs, out, chunks - 1, Y, X, every, (lt,), None, scale=0.5, step_out=SUB)
+
+
+def finish_kernel(done, qs, w2, v2, ss, out, fresh, sem):
+    chunks, tiles = done.shape[:2]
+    pitch = 2 * tiles
+    last_c, last_t = chunks - 1, tiles - 1
+
+    def place(c, t, src, first_line, count, which):
+        return pltpu.make_async_copy(src.reshape(count, SUB, LANES),
+                                     out.at[pl.ds(first_line, count), pl.ds(c * SUB, SUB), pl.ds(t * LANES, LANES)], sem.at[which])
+
+    lines = done.shape[2] // SUB
+    early = lines - LANES
+    copies = [place(c, t, done.at[c, t], 0, lines, c * tiles + t) for c in range(last_c) for t in range(tiles)]
+    copies += [place(last_c, t, done.at[last_c, t, pl.ds(0, early * SUB)], 0, early, last_c * tiles + t) for t in range(tiles)]
     for copy in copies:
         copy.start()
-    for copy in copies:
+
+    def column(f, carry):
+        for kt in range(tiles):
+            rows = pl.ds(kt * LANES * pitch + tiles + last_t, LANES, stride=pitch)
+            block = qs[last_c, last_t, pl.ds((kt * LANES + 1) * PITCH + f, LANES, stride=PITCH), :]
+            block = block + w2[rows, :] * ss[0, last_t, pl.ds(f, 1), :] + v2[rows, :] * ss[1, last_t, pl.ds(f, 1), :]
+            fresh[kt, pl.ds(f, LANES, stride=SUB), :] = (block * 0.5).T
+        return carry
+
+    lax.fori_loop(0, SUB, column, 0, unroll=True)
+    late = [place(last_c, t, fresh.at[t], early, LANES, chunks * tiles + t) for t in range(tiles)]
+    for copy in late:
+        copy.start()
+    for copy in copies + late:
         copy.wait()
 
 
@@ -498,31 +535,34 @@
         sends = pltpu.VMEM((chunks, 2, tiles, SUB, LANES), F32)
         table = lambda count: pltpu.VMEM(((4 * count + 4) * tiles, LANES), F32)
         small = pltpu.VMEM((2, chunks, tiles, SUB, LANES), F32)
-        message = (8 * tiles, LANES)
+        message = (4 * tiles, LANES)
         scratch = [
-            pltpu.VMEM((6, n, n), F32), big, big, big, *([packed] * 17),
-            pltpu.VMEM(message, F32), pltpu.VMEM((parts_x,) + message, F32), pltpu.VMEM((parts_y,) + message, F32),
-            table(parts_x), table(parts_y), sends, sends, pltpu.VMEM((2, chunks, parts_x, tiles, SUB, LANES), F32), pltpu.VMEM((2, chunks, tiles, parts_y, SUB, LANES), F32),
-            pltpu.VMEM((chunks, parts_x, 2, tiles, SUB, LANES), F32),
-            pltpu.VMEM((chunks, tiles, SUB, LANES), F32), pltpu.VMEM((2, tiles, SUB, LANES), F32),
+            pltpu.VMEM((6, n, n), F32), big, big, *([packed] * 15),
+            pltpu.VMEM((2,) + message, F32), pltpu.VMEM((parts_x,) + message, F32), pltpu.VMEM((parts_y,) + message, F32),
+            table(parts_x), table(parts_y), sends, sends,
+            pltpu.VMEM((2, chunks, parts_x, tiles, SUB, LANES), F32), pltpu.VMEM((2, chunks, tiles, parts_y, SUB, LANES), F32),
+            pltpu.VMEM((chunks, parts_x, 2, tiles, SUB, LANES), F32), pltpu.VMEM((chunks, tiles, SUB, LANES), F32),
             pltpu.VMEM((2, tiles, SUB, SUB, LANES), F32), small, small,
-            dma, dma((chunks, tiles)), dma, dma((2,)), dma((2, chunks, tiles)), dma((2, 2, chunks, tiles)), dma((2, chunks)), dma((2,)), dma((2,)),
+            dma, dma((2, chunks)), dma((2, chunks)), dma((2, chunks, tiles)), dma((2,)),
         ]
         in_hbm = pl.BlockSpec(memory_space=pltpu.HBM)
         turned = jnp.transpose(field, (0, 2, 1))
         in_vmem = pl.BlockSpec(memory_space=pltpu.VMEM)
-        tiled = pl.pallas_call(
+        shape = lambda *dims: jax.ShapeDtypeStruct(dims, F32)
+        handed = (shape(chunks, tiles, n * SUB, LANES), shape(chunks, tiles, plane, LANES), shape(n * 2 * tiles, LANES),
+                  shape(n * 2 * tiles, LANES), shape(2, tiles, SUB, LANES))
+        handed = pl.pallas_call(
             functools.partial(adi_kernel, (("row", parts_x), ("col", parts_y)), strides),
-            out_shape=jax.ShapeDtypeStruct((chunks, tiles, n * SUB, LANES), F32),
-            in_specs=[in_hbm] * 7, out_specs=in_vmem, scratch_shapes=scratch,
-            compiler_params=pltpu.CompilerParams(collective_id=0, has_side_effects=True, vmem_limit_bytes=40 * 1024 * 1024),
+            out_shape=handed, in_specs=[in_hbm] * 7, out_specs=(in_vmem,) * len(handed), scratch_shapes=scratch,
+            compiler_params=pltpu.CompilerParams(collective_id=0, has_side_effects=True, vmem_limit_bytes=36 * 1024 * 1024),
             name="adi_steps",
         )(*(pltpu.with_memory_space_constraint(array, pltpu.HBM) for array in (turned,) + coeffs))
         result = pl.pallas_call(
-            unload_kernel, out_shape=jax.ShapeDtypeStruct(turned.shape, F32), in_specs=[in_vmem], out_specs=in_hbm,
-            scratch_shapes=[dma((chunks * tiles,))], compiler_params=pltpu.CompilerParams(vmem_limit_bytes=1024 * 1024),
-            name="unload",
-        )(tiled)
+            finish_kernel, out_shape=jax.ShapeDtypeStruct(turned.shape, F32),
+            in_specs=[in_vmem] * len(handed), out_specs=in_hbm,
+            scratch_shapes=[pltpu.VMEM((tiles, LANES * SUB, LANES), F32), dma((chunks * tiles + tiles,))],
+            compiler_params=pltpu.CompilerParams(vmem_limit_bytes=8 * 1024 * 1024), name="finish",
+        )(*handed)
         return jnp.transpose(result, (0, 2, 1))
 
     return jax.shard_map(local_steps, mesh=mesh, in_specs=(field_spec,) + (coeff_spec,) * 6, out_specs=field_spec, check_vma=False)

time: 39.9 us -> 38.8 us (0.972)
  Pallas kernels: 39.8 us -> 38.7 us
    pallas_call x1, Pallas kernels: 37.8 us -> 36.6 us  [local_steps(): pl.pallas_call(functools.partial(adi_kernel, (('row', parts_x), ('col', p...]
where the time goes in v4:
time: 38.8 us; the launch traced here: 38.7 us
  Pallas kernels  38.7 us (100%)
    pallas_call x1, Pallas kernels, local_steps(): pl.pallas_call(functools.partial(adi_kernel, (('row', parts_x), ('col', p...  36.6 us
    pallas_call x1, Pallas kernels, local_steps(): pl.pallas_call(finish_kernel, out_shape=jax.ShapeDtypeStruct(turned.shape...  2.1 us

profile of v4, /device:TPU:97, one launch (start us, length us, event | category | flops | bytes accessed | tf_op | source)
XLA Modules:
  0.0 38.7 jit_solution(11314861648291276952)
XLA Ops:
  0.0 36.6 %adi_steps.1 = (f32[2,2,2048,128]{3,2,1,0:T(8,128)S(1)}, f32[2,2,2344,128]{3,2,1,0:T(8,128)S(1)}, f32[1024,128]{1,0:T(8,128)S(1)}, f32[1024,128]{1,0:T(8,128)S(1)}, f32[2,2,8,128]{3,2,1,0:T(8,128)S(1)}) custom-call(f32[256,16,256]{2,1,0:T(8,128)} %bitcast.2, f32[256,256]{1,0:T(8,128)} %lower_x.1, f32[256,256]{1,0:T(8,128)} %diag_x.1, f32[256,256]{1,0:T(8,128)} %upper_x.1, ...), custom_call_target="tpu_custom_call" | custom-call | tf_op jit(solution)/shard_map/adi_steps/pallas_call | solution.py:554
  36.6 2.1 %finish.1 = f32[256,16,256]{2,1,0:T(8,128)} custom-call(f32[2,2,2048,128]{3,2,1,0:T(8,128)S(1)} %get-tuple-element.10.done, f32[2,2,2344,128]{3,2,1,0:T(8,128)S(1)} %get-tuple-element.11.qs, f32[1024,128]{1,0:T(8,128)S(1)} %get-tuple-element.12.w2, f32[1024,128]{1,0:T(8,128)S(1)} %get-tuple-element.13.v2, f32[2,2,8,128]{3,2,1,0:T(8,128)S(1)} %get-tuple-element.14.ss), custom_call_target="tpu_custom_call" | custom-call | tf_op jit(solution)/shard_map/finish/pallas_call | solution.py:560

commit v5 on v4

--- a/solution.py
+++ b/solution.py
@@ -11,6 +11,7 @@
 F32 = jnp.float32
 LANES = 128
 SUB = 8
+UNIT = SUB // 2
 PITCH = SUB + 1
 LOGICAL = pl.DeviceIdType.LOGICAL
 X, Y = 0, 1
@@ -18,12 +19,14 @@
 
 def adi_kernel(axes, strides, field, lower_x, diag_x, upper_x, lower_y, diag_y, upper_y, out, qs, w2, v2, ss,
                nat, rs, hs, pa, pb, pc, nd, md, ne, me_, ln, cn, un, an, m2, d2, r0, rn,
-               gs, gc_x, gc_y, red_x, red_y, sx, sy, ex, ey, raw, gt, part, halo_s, halo_r,
+               gs, gc_x, gc_y, red_x, red_y, sx, sy, ex, ey, raw, gt, halo_s, halo_r,
                load_sem, send_sem, recv_x, recv_y, grecv):
     (row_name, parts_x), (col_name, parts_y) = axes
     n = lower_x.shape[0]
     tiles = n // LANES
     chunks = field.shape[1] // SUB
+    parts_of = SUB // UNIT
+    units = chunks * parts_of
     pitch = 2 * tiles
     half = n // 2
     group = 2
@@ -31,6 +34,7 @@
     parts = (parts_x, parts_y)
     home = sum(lax.axis_index(name) * stride for name, stride in strides.items())
     exch = (ex, ey)
+    recv = (recv_x, recv_y)
     send = (sx, sy)
     gather = (gc_x, gc_y)
     reduced = (red_x, red_y)
@@ -45,7 +49,7 @@
 
     def field_piece(c, t):
         return pltpu.make_async_copy(field.at[:, pl.ds(c * SUB, SUB), pl.ds(t * LANES, LANES)],
-                                     out.at[c, t].reshape(n, SUB, LANES), send_sem.at[t, c])
+                                     out.at[c, t].reshape(n, SUB, LANES), send_sem.at[t, c, 0])
 
     for c in range(chunks):
         for t in range(tiles):
@@ -69,25 +73,23 @@
     def each_chunk(body):
         lax.fori_loop(0, chunks, lambda c, carry: (body(c), carry)[1], 0)
 
-    def turn(src, dst, c, axis, to, kts, lts, ends, step_in=PITCH, correct=True, explicit=False, scale=None,
-             before=False, after=False, step_out=PITCH):
+    def turn(src, dst, c, axis, to, base, many, lts, ends=None, step_in=PITCH, step_out=PITCH, correct=True, explicit=False, scale=None):
         def column(g, carry):
             fs = [g * group + u for u in range(group)]
-            for kt in kts:
+            for kt in every:
                 heads, tails = [None] * group, [None] * group
                 for lt in lts:
+                    rows = pl.ds(kt * (LANES * pitch) + (axis * tiles + lt), LANES, stride=pitch)
                     if correct:
-                        rows = pl.ds(kt * (LANES * pitch) + (axis * tiles + lt), LANES, stride=pitch)
                         near, far = w2[rows, :], v2[rows, :]
                     if explicit:
-                        rows = pl.ds(kt * (LANES * pitch) + (axis * tiles + lt), LANES, stride=pitch)
                         own, low, high = 2.0 - pb[rows, :], pa[rows, :], pc[rows, :]
                     if ends:
                         rows = pl.ds(lt * LANES * pitch + to * tiles + kt, LANES, stride=pitch)
                         first_row, last_row = r0[rows, :], rn[rows, :]
                     for u, f in enumerate(fs):
-                        origin = kt * LANES * step_in + (step_in if step_in == PITCH else 0) + f
-                        target = lt * LANES * step_out + (step_out if step_out == PITCH else 0) + f
+                        origin = kt * LANES * step_in + (step_in if step_in == PITCH else 0) + base + f
+                        target = lt * LANES * step_out + (step_out if step_out == PITCH else 0) + base + f
                         block = src[c, lt, pl.ds(origin, LANES, stride=step_in), :]
                         if explicit:
                             block = own * block - (low * src[c, lt, pl.ds(origin - step_in, LANES, stride=step_in), :]
@@ -105,23 +107,18 @@
                             tails[u] = s if tails[u] is None else tails[u] + s
                 if ends:
                     for u, f in enumerate(fs):
-                        if before:
-                            heads[u], tails[u] = heads[u] + part[0, kt, f], tails[u] + part[1, kt, f]
-                        if after:
-                            part[0, kt, f], part[1, kt, f] = heads[u], tails[u]
-                        else:
-                            ends[0][kt, pl.ds(f, 1), :] = jnp.sum(heads[u], axis=0, keepdims=True)
-                            ends[1][kt, pl.ds(f, 1), :] = jnp.sum(tails[u], axis=0, keepdims=True)
+                        ends[0][kt, pl.ds(f, 1), :] = jnp.sum(heads[u], axis=0, keepdims=True)
+                        ends[1][kt, pl.ds(f, 1), :] = jnp.sum(tails[u], axis=0, keepdims=True)
             return carry
 
-        lax.fori_loop(0, SUB // group, column, 0, unroll=True)
+        lax.fori_loop(0, many // group, column, 0, unroll=True)
 
     me_y = pos[Y]
     has_before, has_after = me_y > 0, me_y < parts_y - 1
 
     def halo(side, c, other):
         return pltpu.make_async_remote_copy(
-            src_ref=halo_s.at[side, c], dst_ref=halo_r.at[1 - side, c], send_sem=send_sem.at[side, c], recv_sem=recv_y.at[1, c, 1 - side],
+            src_ref=halo_s.at[side, c], dst_ref=halo_r.at[1 - side, c], send_sem=send_sem.at[side, c, 0], recv_sem=recv_y.at[1, c, 1 - side],
             device_id=device(Y, other), device_id_type=LOGICAL)
 
     def send_halo(c):
@@ -155,7 +152,7 @@
     for c in range(chunks):
         for t in range(tiles):
             field_piece(c, t).wait()
-            turn(out, qs, c, X, Y, every, (t,), None, step_in=SUB, correct=False)
+            turn(out, qs, c, X, Y, 0, SUB, (t,), step_in=SUB, correct=False)
         if c == 0:
             pl.semaphore_wait(barrier, parts_x + parts_y - 2)
         send_halo(c)
@@ -306,93 +303,95 @@
                 put(2 * count + 4 + p, jnp.where(p < me, mu[p], unit))
                 put(3 * count + 4 + p, jnp.where(p < me, unit, jnp.where(p > me, nu[p], nil)))
 
-    def slot(axis, way, c, t, p):
-        return (way, c, p, t) if axis == X else (way, c, t, p)
-
-    def arrival(axis, way, c, t):
-        return recv_x.at[way, c] if axis == X else recv_y.at[way, c, t]
-
-    def publish(axis, stage, c, ts):
+    def publish(axis, stage, c, g):
         count, table, way = parts[axis], reduced[axis], lax.rem(stage, 2)
-        for t in ts:
-            head, tail = exch[axis][slot(axis, way, c, t, pos[axis])], gt[c, t]
+        for t in every:
+            head, tail = exch[axis][way, c, g, pos[axis], t], gt[c, g, t]
             mu = table[pl.ds((2 * count + 2) * tiles + t, 1), :]
             nu = table[pl.ds((2 * count + 3) * tiles + t, 1), :]
-            send[axis][c, 1, t] = tail + mu * head
-            send[axis][c, 0, t] = head + nu * tail
-        some = pl.ds(ts[0], len(ts))
-        there = exch[X].at[way, c, pos[X]] if axis == X else exch[Y].at[way, c, some, pos[Y]]
+            send[axis][c, g, 1, t] = tail + mu * head
+            send[axis][c, g, 0, t] = head + nu * tail
         for other in others(axis):
             sel = jnp.where(other > pos[axis], 1, 0)
             pltpu.make_async_remote_copy(
-                src_ref=send[axis].at[c, sel, some], dst_ref=there,
-                send_sem=send_sem.at[axis, c], recv_sem=arrival(axis, way, c, ts[0]),
+                src_ref=send[axis].at[c, g, sel], dst_ref=exch[axis].at[way, c, g, pos[axis]],
+                send_sem=send_sem.at[axis, c, g], recv_sem=recv[axis].at[way, c, g],
                 device_id=device(axis, other), device_id_type=LOGICAL).start()
 
-    def combine(axis, stage, c, ts):
-        count, table, way = parts[axis], reduced[axis], lax.rem(stage, 2)
-        for t in ts:
+    def combine(axis, way, c, g):
+        count, table = parts[axis], reduced[axis]
+        for t in every:
             for side in range(2):
                 base = side * (count + 1) * tiles + t
-                total = table[pl.ds(base + count * tiles, 1), :] * gt[c, t]
+                total = table[pl.ds(base + count * tiles, 1), :] * gt[c, g, t]
                 for p in range(count):
-                    total = total + table[pl.ds(base + p * tiles, 1), :] * exch[axis][slot(axis, way, c, t, p)]
+                    total = total + table[pl.ds(base + p * tiles, 1), :] * exch[axis][way, c, g, p, t]
                 ss[side, t] = total
 
-    def neighbours(axis, stage, c, ts):
+    def neighbours(axis, stage, c, g):
         way = lax.rem(stage, 2)
-        some = pl.ds(0, parts[axis] - 1)
-        arrived = exch[X].at[way, c, some] if axis == X else exch[Y].at[way, c, pl.ds(ts[0], len(ts)), some]
-        pltpu.make_async_copy(arrived, arrived, arrival(axis, way, c, ts[0])).wait()
-        if ts[-1] == tiles - 1:
-            sent = arrived if axis == X else exch[Y].at[way, c, :, some]
-            pltpu.make_async_copy(sent, sent, send_sem.at[axis, c]).wait()
-        combine(axis, stage, c, ts)
-
-    def publish_raw(c):
-        for t in range(tiles):
-            raw[c, pos[X], 0, t] = exch[X][slot(X, 0, c, t, pos[X])]
-            raw[c, pos[X], 1, t] = gt[c, t]
+        arrived = exch[axis].at[way, c, g, pl.ds(0, parts[axis] - 1)]
+        pltpu.make_async_copy(arrived, arrived, recv[axis].at[way, c, g]).wait()
+        pltpu.make_async_copy(arrived, arrived, send_sem.at[axis, c, g]).wait()
+        combine(axis, way, c, g)
+
+    def publish_raw(c, g):
+        for t in every:
+            raw[c, g, pos[X], 0, t] = exch[X][0, c, g, pos[X], t]
+            raw[c, g, pos[X], 1, t] = gt[c, g, t]
         for other in others(X):
             pltpu.make_async_remote_copy(
-                src_ref=raw.at[c, pos[X]], dst_ref=raw.at[c, pos[X]], send_sem=send_sem.at[X, c], recv_sem=recv_x.at[0, c],
+                src_ref=raw.at[c, g, pos[X]], dst_ref=raw.at[c, g, pos[X]], send_sem=send_sem.at[X, c, g], recv_sem=recv_x.at[0, c, g],
                 device_id=device(X, other), device_id_type=LOGICAL).start()
 
-    def neighbours_raw(c):
+    def neighbours_raw(c, g):
         count = parts_x
-        arrived = raw.at[c, pl.ds(0, count - 1)]
-        pltpu.make_async_copy(arrived, arrived, recv_x.at[0, c]).wait()
-        pltpu.make_async_copy(arrived, arrived, send_sem.at[X, c]).wait()
-        for t in range(tiles):
+        arrived = raw.at[c, g, pl.ds(0, count - 1)]
+        pltpu.make_async_copy(arrived, arrived, recv_x.at[0, c, g]).wait()
+        pltpu.make_async_copy(arrived, arrived, send_sem.at[X, c, g]).wait()
+        for t in every:
             for p in range(count):
                 on_head = red_x[pl.ds((2 * count + 4 + p) * tiles + t, 1), :]
                 on_tail = red_x[pl.ds((3 * count + 4 + p) * tiles + t, 1), :]
-                exch[X][slot(X, 0, c, t, p)] = on_head * raw[c, p, 0, t] + on_tail * raw[c, p, 1, t]
-        combine(X, 0, c, every)
+                exch[X][0, c, g, p, t] = on_head * raw[c, g, p, 0, t] + on_tail * raw[c, g, p, 1, t]
+        combine(X, 0, c, g)
 
     def solve_block(axis, minus):
         def coef(array, k, t):
             return array[pl.ds(k * pitch + axis * tiles + t, 1), :]
 
-        def forward(k, state):
-            ups, downs = list(state[0]), list(state[1])
-            r = n - 1 - k
-            for t in range(tiles):
-                up, down = coef(ln, k, t), coef(un, r, t)
-                for c in range(chunks):
-                    s = c * tiles + t
-                    ups[s] = rs[c, t, slab(k), :] + up * ups[s]
-                    hs[c, t, slab(k), :] = ups[s]
-                    downs[s] = rs[c, t, slab(r), :] + down * downs[s]
-                    hs[c, t, slab(r), :] = downs[s]
-            return tuple(ups), tuple(downs)
+        def walk(first, sign, count, visit, state):
+            def block(g, state):
+                line = first + sign * unroll * g
+                row, coef_row = (line + 1) * PITCH, line * pitch + axis * tiles
+
+                def one(u, state):
+                    at = lambda array, t: array[pl.ds(coef_row + t + u * (sign * pitch), 1), :]
+                    return visit(pl.ds(row + u * (sign * PITCH), SUB), at, state)
+
+                return lax.fori_loop(0, min(count, unroll), one, state, unroll=True)
+
+            return lax.fori_loop(0, max(count // unroll, 1), block, state)
+
+        def eliminate(mult):
+            def visit(here, at, state):
+                values = list(state)
+                for t in every:
+                    factor = at(mult, t)
+                    for c in range(chunks):
+                        s = c * tiles + t
+                        values[s] = rs[c, t, here, :] + factor * values[s]
+                        hs[c, t, here, :] = values[s]
+                return tuple(values)
+            return visit
 
         init = tuple(blank for _ in cells)
-        ups, downs = lax.fori_loop(0, half, forward, (init, init), unroll=unroll)
+        ups = walk(0, 1, half, eliminate(ln), init)
+        downs = walk(n - 1, -1, half, eliminate(un), init)
         lo, hi = half - 1, half
 
-        def place(c, t, k, value):
-            qs[c, t, slab(k), :] = value - rs[c, t, slab(k), :] if minus else value
+        def place(c, t, here, value):
+            qs[c, t, here, :] = value - rs[c, t, here, :] if minus else value
 
         low_s, high_s = [], []
         for s, (c, t) in enumerate(cells):
@@ -402,47 +401,47 @@
             s_lo = kappa * (coef(m2, lo, t) * ups[s] + c_lo * h_hi)
             low_s.append(s_lo)
             high_s.append(h_hi + a_hi * s_lo)
-            place(c, t, lo, low_s[s])
-            place(c, t, hi, high_s[s])
-
-        def backward(step, state):
-            lows, highs = list(state[0]), list(state[1])
-            k, r = half - 1 - step, half + step
-            for t in range(tiles):
-                m_low, c_low, m_high, a_high = coef(m2, k, t), coef(cn, k, t), coef(d2, r, t), coef(an, r, t)
-                for c in range(chunks):
-                    s = c * tiles + t
-                    lows[s] = m_low * hs[c, t, slab(k), :] + c_low * lows[s]
-                    place(c, t, k, lows[s])
-                    highs[s] = m_high * hs[c, t, slab(r), :] + a_high * highs[s]
-                    place(c, t, r, highs[s])
-            return tuple(lows), tuple(highs)
-
-        state = lax.fori_loop(1, unroll, backward, (tuple(low_s), tuple(high_s)), unroll=True)
-        lax.fori_loop(unroll, half, backward, state, unroll=unroll)
-
-    def each_chunk(body):
-        lax.fori_loop(0, chunks, lambda c, carry: (body(c), carry)[1], 0)
-
-    def ends_of(axis, stage, c):
-        way = lax.rem(stage, 2)
-        return exch[X].at[way, c, pos[X]] if axis == X else exch[Y].at[way, c, :, pos[Y]], gt.at[c]
+            place(c, t, slab(lo), low_s[s])
+            place(c, t, slab(hi), high_s[s])
+
+        def substitute(scale, mult):
+            def visit(here, at, state):
+                values = list(state)
+                for t in every:
+                    own, factor = at(scale, t), at(mult, t)
+                    for c in range(chunks):
+                        s = c * tiles + t
+                        values[s] = own * hs[c, t, here, :] + factor * values[s]
+                        place(c, t, here, values[s])
+                return tuple(values)
+            return visit
+
+        for first, sign, visit, state in ((lo, -1, substitute(m2, cn), low_s), (hi, 1, substitute(d2, an), high_s)):
+            state = walk(first + sign, sign, unroll - 1, visit, tuple(state))
+            walk(first + sign * unroll, sign, half - unroll, visit, state)
+
+    def each_unit(body, count=units):
+        lax.fori_loop(0, count, lambda u, carry: (body(u // parts_of, lax.rem(u, parts_of)), carry)[1], 0)
+
+    def ends_of(axis, stage, c, g):
+        return exch[axis].at[lax.rem(stage, 2), c, g, pos[axis]], gt.at[c, g]
 
     def start_x(c):
+        def unit(g, carry):
+            turn(qs, rs, c, Y, X, g * UNIT, UNIT, every, ends_of(X, 0, c, g), correct=False, explicit=True)
+            publish_raw(c, g)
+            return carry
+
         await_halo(c)
-        turn(qs, rs, c, Y, X, every, every, ends_of(X, 0, c), correct=False, explicit=True)
-        publish_raw(c)
-
-    def to_y(stage, c):
-        for kt in every:
-            turn(qs, rs, c, X, Y, (kt,), every, ends_of(Y, stage, c))
-            publish(Y, stage, c, (kt,))
-
-    def to_x(stage, c):
-        for lt in every:
-            neighbours(Y, stage, c, (lt,))
-            turn(qs, rs, c, Y, X, every, (lt,), ends_of(X, stage + 1, c), before=lt > 0, after=lt < tiles - 1)
-        publish(X, stage + 1, c, every)
+        lax.fori_loop(0, parts_of, unit, 0)
+
+    def onward(axis, stage, to, to_stage):
+        def unit(c, g):
+            neighbours(axis, stage, c, g)
+            turn(qs, rs, c, axis, to, g * UNIT, UNIT, every, ends_of(to, to_stage, c, g))
+            publish(to, to_stage, c, g)
+
+        each_unit(unit)
 
     each_chunk(start_x)
     solve_block(X, True)
@@ -453,67 +452,58 @@
     sent = gc_y.at[pl.ds(0, parts_y - 1)]
     pltpu.make_async_copy(sent, sent, load_sem).wait()
 
-    def first_to_y(c):
-        neighbours_raw(c)
-        to_y(0, c)
-
-    each_chunk(first_to_y)
+    def first_to_y(c, g):
+        neighbours_raw(c, g)
+        turn(qs, rs, c, X, Y, g * UNIT, UNIT, every, ends_of(Y, 0, c, g))
+        publish(Y, 0, c, g)
+
+    each_unit(first_to_y)
 
     def step(stage, carry):
-        def onward(c):
-            neighbours(X, stage, c, every)
-            to_y(stage, c)
-
         solve_block(Y, True)
-        each_chunk(lambda c: to_x(stage - 1, c))
+        onward(Y, stage - 1, X, stage)
         solve_block(X, True)
-        each_chunk(onward)
+        onward(X, stage, Y, stage)
         return carry
 
     lax.fori_loop(1, STEPS, step, 0)
     solve_block(Y, False)
 
-    def finish(c):
-        for lt in every:
-            neighbours(Y, STEPS - 1, c, (lt,))
-            turn(qs, out, c, Y, X, every, (lt,), None, scale=0.5, step_out=SUB)
-
-    lax.fori_loop(0, chunks - 1, lambda c, carry: (finish(c), carry)[1], 0)
-    for lt in every:
-        neighbours(Y, STEPS - 1, chunks - 1, (lt,))
-        if lt < tiles - 1:
-            turn(qs, out, chunks - 1, Y, X, every, (lt,), None, scale=0.5, step_out=SUB)
+    def finish(c, g):
+        neighbours(Y, STEPS - 1, c, g)
+        turn(qs, out, c, Y, X, g * UNIT, UNIT, every, scale=0.5, step_out=SUB)
+
+    each_unit(finish, units - 1)
+    neighbours(Y, STEPS - 1, chunks - 1, parts_of - 1)
 
 
 def finish_kernel(done, qs, w2, v2, ss, out, fresh, sem):
     chunks, tiles = done.shape[:2]
-    pitch = 2 * tiles
-    last_c, last_t = chunks - 1, tiles - 1
-
-    def place(c, t, src, first_line, count, which):
-        return pltpu.make_async_copy(src.reshape(count, SUB, LANES),
-                                     out.at[pl.ds(first_line, count), pl.ds(c * SUB, SUB), pl.ds(t * LANES, LANES)], sem.at[which])
-
-    lines = done.shape[2] // SUB
-    early = lines - LANES
-    copies = [place(c, t, done.at[c, t], 0, lines, c * tiles + t) for c in range(last_c) for t in range(tiles)]
-    copies += [place(last_c, t, done.at[last_c, t, pl.ds(0, early * SUB)], 0, early, last_c * tiles + t) for t in range(tiles)]
+    lines, pitch, last = done.shape[2] // SUB, 2 * tiles, chunks - 1
+    base = SUB - UNIT
+
+    def place(c, t, src):
+        return pltpu.make_async_copy(src.reshape(lines, SUB, LANES), out.at[:, pl.ds(c * SUB, SUB), pl.ds(t * LANES, LANES)],
+                                     sem.at[c * tiles + t])
+
+    copies = [place(c, t, done.at[c, t]) for c in range(last) for t in range(tiles)]
     for copy in copies:
         copy.start()
-
-    def column(f, carry):
-        for kt in range(tiles):
-            rows = pl.ds(kt * LANES * pitch + tiles + last_t, LANES, stride=pitch)
-            block = qs[last_c, last_t, pl.ds((kt * LANES + 1) * PITCH + f, LANES, stride=PITCH), :]
-            block = block + w2[rows, :] * ss[0, last_t, pl.ds(f, 1), :] + v2[rows, :] * ss[1, last_t, pl.ds(f, 1), :]
-            fresh[kt, pl.ds(f, LANES, stride=SUB), :] = (block * 0.5).T
-        return carry
-
-    lax.fori_loop(0, SUB, column, 0, unroll=True)
-    late = [place(last_c, t, fresh.at[t], early, LANES, chunks * tiles + t) for t in range(tiles)]
-    for copy in late:
-        copy.start()
-    for copy in copies + late:
+    for kt in range(tiles):
+        fresh[kt] = done[last, kt]
+
+        def column(f, carry):
+            for lt in range(tiles):
+                rows = pl.ds(kt * LANES * pitch + tiles + lt, LANES, stride=pitch)
+                block = qs[last, lt, pl.ds((kt * LANES + 1) * PITCH + base + f, LANES, stride=PITCH), :]
+                block = block + w2[rows, :] * ss[0, lt, pl.ds(f, 1), :] + v2[rows, :] * ss[1, lt, pl.ds(f, 1), :]
+                fresh[kt, pl.ds(lt * LANES * SUB + base + f, LANES, stride=SUB), :] = (block * 0.5).T
+            return carry
+
+        lax.fori_loop(0, UNIT, column, 0, unroll=True)
+        copies.append(place(last, kt, fresh.at[kt]))
+        copies[-1].start()
+    for copy in copies:
         copy.wait()
 
 
@@ -532,25 +522,25 @@
         plane = -(-((n + 2) * PITCH - SUB) // (4 * SUB)) * 4 * SUB + SUB
         big = pltpu.VMEM((chunks, tiles, plane, LANES), F32)
         dma = pltpu.SemaphoreType.DMA
-        sends = pltpu.VMEM((chunks, 2, tiles, SUB, LANES), F32)
+        parts_of = SUB // UNIT
+        sends = pltpu.VMEM((chunks, parts_of, 2, tiles, UNIT, LANES), F32)
+        line = lambda count: pltpu.VMEM((2, chunks, parts_of, count, tiles, UNIT, LANES), F32)
         table = lambda count: pltpu.VMEM(((4 * count + 4) * tiles, LANES), F32)
         small = pltpu.VMEM((2, chunks, tiles, SUB, LANES), F32)
         message = (4 * tiles, LANES)
         scratch = [
             pltpu.VMEM((6, n, n), F32), big, big, *([packed] * 15),
             pltpu.VMEM((2,) + message, F32), pltpu.VMEM((parts_x,) + message, F32), pltpu.VMEM((parts_y,) + message, F32),
-            table(parts_x), table(parts_y), sends, sends,
-            pltpu.VMEM((2, chunks, parts_x, tiles, SUB, LANES), F32), pltpu.VMEM((2, chunks, tiles, parts_y, SUB, LANES), F32),
-            pltpu.VMEM((chunks, parts_x, 2, tiles, SUB, LANES), F32), pltpu.VMEM((chunks, tiles, SUB, LANES), F32),
-            pltpu.VMEM((2, tiles, SUB, SUB, LANES), F32), small, small,
-            dma, dma((2, chunks)), dma((2, chunks)), dma((2, chunks, tiles)), dma((2,)),
+            table(parts_x), table(parts_y), sends, sends, line(parts_x), line(parts_y),
+            pltpu.VMEM((chunks, parts_of, parts_x, 2, tiles, UNIT, LANES), F32), pltpu.VMEM((chunks, parts_of, tiles, UNIT, LANES), F32),
+            small, small, dma, dma((2, chunks, parts_of)), dma((2, chunks, parts_of)), dma((2, chunks, parts_of)), dma((2,)),
         ]
         in_hbm = pl.BlockSpec(memory_space=pltpu.HBM)
         turned = jnp.transpose(field, (0, 2, 1))
         in_vmem = pl.BlockSpec(memory_space=pltpu.VMEM)
         shape = lambda *dims: jax.ShapeDtypeStruct(dims, F32)
         handed = (shape(chunks, tiles, n * SUB, LANES), shape(chunks, tiles, plane, LANES), shape(n * 2 * tiles, LANES),
-                  shape(n * 2 * tiles, LANES), shape(2, tiles, SUB, LANES))
+                  shape(n * 2 * tiles, LANES), shape(2, tiles, UNIT, LANES))
         handed = pl.pallas_call(
             functools.partial(adi_kernel, (("row", parts_x), ("col", parts_y)), strides),
             out_shape=handed, in_specs=[in_hbm] * 7, out_specs=(in_vmem,) * len(handed), scratch_shapes=scratch,
@@ -560,7 +550,7 @@
         result = pl.pallas_call(
             finish_kernel, out_shape=jax.ShapeDtypeStruct(turned.shape, F32),
             in_specs=[in_vmem] * len(handed), out_specs=in_hbm,
-            scratch_shapes=[pltpu.VMEM((tiles, LANES * SUB, LANES), F32), dma((chunks * tiles + tiles,))],
+            scratch_shapes=[pltpu.VMEM((tiles, n * SUB, LANES), F32), dma((chunks * tiles,))],
             compiler_params=pltpu.CompilerParams(vmem_limit_bytes=8 * 1024 * 1024), name="finish",
         )(*handed)
         return jnp.transpose(result, (0, 2, 1))

time: 38.8 us -> 37.3 us (0.961)
  Pallas kernels: 38.7 us -> 37.2 us
    pallas_call x1, Pallas kernels: 36.6 us -> 35.2 us  [local_steps(): pl.pallas_call(functools.partial(adi_kernel, (('row', parts_x), ('col', p...]
where the time goes in v5:
time: 37.3 us
  Pallas kernels  37.2 us (100%)
    pallas_call x1, Pallas kernels, local_steps(): pl.pallas_call(functools.partial(adi_kernel, (('row', parts_x), ('col', p...  35.2 us
    pallas_call x1, Pallas kernels, local_steps(): pl.pallas_call(finish_kernel, out_shape=jax.ShapeDtypeStruct(turned.shape...  2.08 us

profile of v5, /device:TPU:97, one launch (start us, length us, event | category | flops | bytes accessed | tf_op | source)
XLA Modules:
  0.0 37.3 jit_solution(1218207981266003601)
XLA Ops:
  0.0 35.2 %adi_steps.1 = (f32[2,2,2048,128]{3,2,1,0:T(8,128)S(1)}, f32[2,2,2344,128]{3,2,1,0:T(8,128)S(1)}, f32[1024,128]{1,0:T(8,128)S(1)}, f32[1024,128]{1,0:T(8,128)S(1)}, f32[2,2,4,128]{3,2,1,0:T(4,128)S(1)}) custom-call(f32[256,16,256]{2,1,0:T(8,128)} %bitcast.2, f32[256,256]{1,0:T(8,128)} %lower_x.1, f32[256,256]{1,0:T(8,128)} %diag_x.1, f32[256,256]{1,0:T(8,128)} %upper_x.1, ...), custom_call_target="tpu_custom_call" | custom-call | tf_op jit(solution)/shard_map/adi_steps/pallas_call | solution.py:544
  35.2 2.1 %finish.1 = f32[256,16,256]{2,1,0:T(8,128)} custom-call(f32[2,2,2048,128]{3,2,1,0:T(8,128)S(1)} %get-tuple-element.10.done, f32[2,2,2344,128]{3,2,1,0:T(8,128)S(1)} %get-tuple-element.11.qs, f32[1024,128]{1,0:T(8,128)S(1)} %get-tuple-element.12.w2, f32[1024,128]{1,0:T(8,128)S(1)} %get-tuple-element.13.v2, f32[2,2,4,128]{3,2,1,0:T(4,128)S(1)} %get-tuple-element.14.ss), custom_call_target="tpu_custom_call" | custom-call | tf_op jit(solution)/shard_map/finish/pallas_call | solution.py:550

commit v6 on v5

--- a/solution.py
+++ b/solution.py
@@ -19,8 +19,8 @@
 
 def adi_kernel(axes, strides, field, lower_x, diag_x, upper_x, lower_y, diag_y, upper_y, out, qs, w2, v2, ss,
                nat, rs, hs, pa, pb, pc, nd, md, ne, me_, ln, cn, un, an, m2, d2, r0, rn,
-               gs, gc_x, gc_y, red_x, red_y, sx, sy, ex, ey, raw, gt, halo_s, halo_r,
-               load_sem, send_sem, recv_x, recv_y, grecv):
+               gs, gc, red_x, red_y, sx, sy, ex, ey, raw, gt, halo_s, halo_r,
+               load_sem, late_sem, send_sem, recv_x, recv_y, gather_sem):
     (row_name, parts_x), (col_name, parts_y) = axes
     n = lower_x.shape[0]
     tiles = n // LANES
@@ -29,14 +29,12 @@
     units = chunks * parts_of
     pitch = 2 * tiles
     half = n // 2
-    group = 2
     pos = (lax.axis_index(row_name), lax.axis_index(col_name))
     parts = (parts_x, parts_y)
     home = sum(lax.axis_index(name) * stride for name, stride in strides.items())
     exch = (ex, ey)
     recv = (recv_x, recv_y)
     send = (sx, sy)
-    gather = (gc_x, gc_y)
     reduced = (red_x, red_y)
 
     def device(axis, other):
@@ -47,15 +45,24 @@
         offs = sorted(range(1, count), key=lambda off: -min(off, count - off))
         return [lax.rem(pos[axis] + off, count) for off in offs]
 
-    def field_piece(c, t):
-        return pltpu.make_async_copy(field.at[:, pl.ds(c * SUB, SUB), pl.ds(t * LANES, LANES)],
-                                     out.at[c, t].reshape(n, SUB, LANES), send_sem.at[t, c, 0])
+    def field_piece(c, t, first=0, count=n):
+        return pltpu.make_async_copy(field.at[pl.ds(first, count), pl.ds(c * SUB, SUB), pl.ds(t * LANES, LANES)],
+                                     out.at[c, t, pl.ds(first * SUB, count * SUB)].reshape(count, SUB, LANES), send_sem.at[t, c, 0])
+
+    def load_field(c):
+        for t in range(tiles):
+            for first in range(0, n, LANES):
+                field_piece(c, t, first, LANES).start()
+
+    def load_coefficients(axis):
+        for slot, ref in enumerate(((lower_x, diag_x, upper_x), (lower_y, diag_y, upper_y))[axis]):
+            pltpu.make_async_copy(ref, nat.at[3 * axis + slot], (load_sem, late_sem)[axis]).start()
 
     for c in range(chunks):
-        for t in range(tiles):
-            field_piece(c, t).start()
-    for slot, ref in enumerate((lower_x, diag_x, upper_x, lower_y, diag_y, upper_y)):
-        pltpu.make_async_copy(ref, nat.at[slot], load_sem).start()
+        if c == chunks - 1:
+            load_coefficients(X)
+        load_field(c)
+    load_coefficients(Y)
 
     halo_r[...] = jnp.zeros_like(halo_r)
     barrier = pltpu.get_barrier_semaphore()
@@ -73,7 +80,10 @@
     def each_chunk(body):
         lax.fori_loop(0, chunks, lambda c, carry: (body(c), carry)[1], 0)
 
-    def turn(src, dst, c, axis, to, base, many, lts, ends=None, step_in=PITCH, step_out=PITCH, correct=True, explicit=False, scale=None):
+    def turn(src, dst, c, axis, to, base, many, lts, ends=None, step_in=PITCH, step_out=PITCH, correct=True, explicit=False, scale=None,
+             g_ss=0):
+        group = 2
+
         def column(g, carry):
             fs = [g * group + u for u in range(group)]
             for kt in every:
@@ -95,7 +105,7 @@
                             block = own * block - (low * src[c, lt, pl.ds(origin - step_in, LANES, stride=step_in), :]
                                                    + high * src[c, lt, pl.ds(origin + step_in, LANES, stride=step_in), :])
                         if correct:
-                            block = block + near * ss[0, lt, pl.ds(f, 1), :] + far * ss[1, lt, pl.ds(f, 1), :]
+                            block = block + near * ss[g_ss, 0, lt, pl.ds(f, 1), :] + far * ss[g_ss, 1, lt, pl.ds(f, 1), :]
                         if scale is not None:
                             block = block * scale
                         flipped = block.T
@@ -149,19 +159,28 @@
             qs[c, t, slab(-1), :] = halo_r[0, c, t]
             qs[c, t, slab(n), :] = halo_r[1, c, t]
 
+    def pack_x():
+        some = nat.at[pl.ds(0, 3)]
+        pltpu.make_async_copy(some, some, load_sem).wait()
+        for t in range(tiles):
+            cols = pl.ds(t * LANES, LANES)
+            pa[pl.ds(t, n, stride=pitch), :] = nat[0, :, cols]
+            pb[pl.ds(t, n, stride=pitch), :] = nat[1, :, cols] + 1.0
+            pc[pl.ds(t, n, stride=pitch), :] = nat[2, :, cols]
+
     for c in range(chunks):
+        if c == chunks - 1:
+            pack_x()
         for t in range(tiles):
             field_piece(c, t).wait()
             turn(out, qs, c, X, Y, 0, SUB, (t,), step_in=SUB, correct=False)
         if c == 0:
             pl.semaphore_wait(barrier, parts_x + parts_y - 2)
         send_halo(c)
-    pltpu.make_async_copy(nat, nat, load_sem).wait()
+    some = nat.at[pl.ds(3, 3)]
+    pltpu.make_async_copy(some, some, late_sem).wait()
     for t in range(tiles):
         cols = pl.ds(t * LANES, LANES)
-        pa[pl.ds(t, n, stride=pitch), :] = nat[0, :, cols]
-        pb[pl.ds(t, n, stride=pitch), :] = nat[1, :, cols] + 1.0
-        pc[pl.ds(t, n, stride=pitch), :] = nat[2, :, cols]
         for s in range(tiles):
             rows = pl.ds(s * LANES, LANES)
             dest = pl.ds(t * LANES * pitch + tiles + s, LANES, stride=pitch)
@@ -169,7 +188,7 @@
             pb[dest, :] = nat[4, rows, cols].T + 1.0
             pc[dest, :] = nat[5, rows, cols].T
 
-    unroll, long = 8, 16
+    long, deep = 16, 16
     zero = jnp.zeros((pitch, LANES), F32)
     one = jnp.ones((pitch, LANES), F32)
 
@@ -179,19 +198,24 @@
     def pivots(g, state):
         dp, dq, c_prev, ep, eq, a_next = state
         h = n // long - 1 - g
-        for u in range(long):
-            up, down = at_row(g, u), at_row(h, long - 1 - u)
-            nd[up, :] = dp
-            new = pb[up, :] * dp - (pa[up, :] * c_prev) * dq
-            md[up, :] = new
-            dp, dq, c_prev = new, dp, pc[up, :]
-            ne[down, :] = ep
-            new = pb[down, :] * ep - (a_next * pc[down, :]) * eq
-            me_[down, :] = new
-            ep, eq, a_next = new, ep, pa[down, :]
-            if u % 8 == 3:
+        for u in range(0, long, 2):
+            up, next_up = at_row(g, u), at_row(g, u + 1)
+            b, t = pb[up, :], pa[up, :] * c_prev
+            next_b, next_t = pb[next_up, :], pa[next_up, :] * pc[up, :]
+            new = b * dp - t * dq
+            newer = (next_b * b - next_t) * dp - (next_b * t) * dq
+            nd[up, :], md[up, :], nd[next_up, :], md[next_up, :] = dp, new, new, newer
+            dp, dq, c_prev = newer, new, pc[next_up, :]
+            down, next_down = at_row(h, long - 1 - u), at_row(h, long - 2 - u)
+            b, t = pb[down, :], a_next * pc[down, :]
+            next_b, next_t = pb[next_down, :], pa[down, :] * pc[next_down, :]
+            new = b * ep - t * eq
+            newer = (next_b * b - next_t) * ep - (next_b * t) * eq
+            ne[down, :], me_[down, :], ne[next_down, :], me_[next_down, :] = ep, new, new, newer
+            ep, eq, a_next = newer, new, pa[next_down, :]
+            if u % 8 == 2:
                 scale_d, scale_e = 1.0 / dp, 1.0 / ep
-            if u % 8 == 7:
+            if u % 8 == 6:
                 dp, dq, ep, eq = dp * scale_d, dq * scale_d, ep * scale_e, eq * scale_e
         return dp, dq, c_prev, ep, eq, a_next
 
@@ -245,20 +269,32 @@
     lax.fori_loop(0, n // long, products,
                   (-pa[first, :] * d2[first, :], d_first, -pc[last, :] * m2[last, :], m_last, one, one))
 
-    for axis in (X, Y):
+    def block_ends(axis):
         for q, (ref, line) in enumerate(((w2, 0), (w2, n - 1), (v2, 0), (v2, n - 1))):
-            gs[axis, pl.ds(q * tiles, tiles), :] = -0.5 * ref[pl.ds(line * pitch + axis * tiles, tiles), :]
-        gather[axis][pos[axis]] = gs[axis]
-        for other in others(axis):
+            yield q * tiles, -0.5 * ref[pl.ds(line * pitch + axis * tiles, tiles), :]
+
+    for row, values in block_ends(X):
+        for t in every:
+            raw[0, 0, pos[X], 2 * tiles + (row + t) // UNIT, pl.ds((row + t) % UNIT, 1), :] = values[t:t + 1]
+
+    def spread_y():
+        for row, values in block_ends(Y):
+            gs[pl.ds(row, tiles), :] = values
+        gc[pos[Y]] = gs[...]
+        for other in others(Y):
             pltpu.make_async_remote_copy(
-                src_ref=gs.at[axis], dst_ref=gather[axis].at[pos[axis]], send_sem=load_sem, recv_sem=grecv.at[axis],
-                device_id=device(axis, other), device_id_type=LOGICAL).start()
+                src_ref=gs, dst_ref=gc.at[pos[Y]], send_sem=load_sem, recv_sem=gather_sem,
+                device_id=device(Y, other), device_id_type=LOGICAL).start()
 
     def reduce_lines(axis):
         count, me = parts[axis], pos[axis]
-        arrived = gather[axis].at[pl.ds(0, count - 1)]
-        pltpu.make_async_copy(arrived, arrived, grecv.at[axis]).wait()
-        part = lambda p, q: gather[axis][p, pl.ds(q * tiles, tiles), :]
+        if axis == Y:
+            arrived = gc.at[pl.ds(0, count - 1)]
+            pltpu.make_async_copy(arrived, arrived, gather_sem).wait()
+            pltpu.make_async_copy(arrived, arrived, load_sem).wait()
+            part = lambda p, q: gc[p, pl.ds(q * tiles, tiles), :]
+        else:
+            part = lambda p, q: raw[0, 0, p, 2 * tiles + q * tiles // UNIT, pl.ds(q * tiles % UNIT, tiles), :]
         nil = jnp.zeros((tiles, LANES), F32)
         unit = jnp.ones((tiles, LANES), F32)
         mu, rho, tau = [None] * count, [None] * count, [None] * count
@@ -318,7 +354,7 @@
                 send_sem=send_sem.at[axis, c, g], recv_sem=recv[axis].at[way, c, g],
                 device_id=device(axis, other), device_id_type=LOGICAL).start()
 
-    def combine(axis, way, c, g):
+    def combine(axis, way, c, g, g_ss=0):
         count, table = parts[axis], reduced[axis]
         for t in every:
             for side in range(2):
@@ -326,34 +362,46 @@
                 total = table[pl.ds(base + count * tiles, 1), :] * gt[c, g, t]
                 for p in range(count):
                     total = total + table[pl.ds(base + p * tiles, 1), :] * exch[axis][way, c, g, p, t]
-                ss[side, t] = total
-
-    def neighbours(axis, stage, c, g):
+                ss[g_ss, side, t] = total
+
+    def neighbours(axis, stage, c, g, g_ss=0):
         way = lax.rem(stage, 2)
         arrived = exch[axis].at[way, c, g, pl.ds(0, parts[axis] - 1)]
         pltpu.make_async_copy(arrived, arrived, recv[axis].at[way, c, g]).wait()
         pltpu.make_async_copy(arrived, arrived, send_sem.at[axis, c, g]).wait()
-        combine(axis, way, c, g)
+        combine(axis, way, c, g, g_ss)
 
     def publish_raw(c, g):
         for t in every:
-            raw[c, g, pos[X], 0, t] = exch[X][0, c, g, pos[X], t]
-            raw[c, g, pos[X], 1, t] = gt[c, g, t]
-        for other in others(X):
-            pltpu.make_async_remote_copy(
-                src_ref=raw.at[c, g, pos[X]], dst_ref=raw.at[c, g, pos[X]], send_sem=send_sem.at[X, c, g], recv_sem=recv_x.at[0, c, g],
-                device_id=device(X, other), device_id_type=LOGICAL).start()
+            raw[c, g, pos[X], t] = exch[X][0, c, g, pos[X], t]
+            raw[c, g, pos[X], tiles + t] = gt[c, g, t]
+
+        def send_raw(c, g, some):
+            for other in others(X):
+                pltpu.make_async_remote_copy(
+                    src_ref=raw.at[c, g, pos[X], some], dst_ref=raw.at[c, g, pos[X], some],
+                    send_sem=send_sem.at[X, c, g], recv_sem=recv_x.at[0, c, g], device_id=device(X, other), device_id_type=LOGICAL).start()
+
+        @pl.when((c == 0) & (g == 0))
+        def _():
+            send_raw(0, 0, pl.ds(0, raw.shape[3]))
+
+        @pl.when((c > 0) | (g > 0))
+        def _():
+            send_raw(c, g, pl.ds(0, 2 * tiles))
+
+    def await_raw(c, g, blocks):
+        arrived = raw.at[c, g, pl.ds(0, parts_x - 1), pl.ds(0, blocks)]
+        pltpu.make_async_copy(arrived, arrived, recv_x.at[0, c, g]).wait()
+        pltpu.make_async_copy(arrived, arrived, send_sem.at[X, c, g]).wait()
 
     def neighbours_raw(c, g):
         count = parts_x
-        arrived = raw.at[c, g, pl.ds(0, count - 1)]
-        pltpu.make_async_copy(arrived, arrived, recv_x.at[0, c, g]).wait()
-        pltpu.make_async_copy(arrived, arrived, send_sem.at[X, c, g]).wait()
         for t in every:
             for p in range(count):
                 on_head = red_x[pl.ds((2 * count + 4 + p) * tiles + t, 1), :]
                 on_tail = red_x[pl.ds((3 * count + 4 + p) * tiles + t, 1), :]
-                exch[X][0, c, g, p, t] = on_head * raw[c, g, p, 0, t] + on_tail * raw[c, g, p, 1, t]
+                exch[X][0, c, g, p, t] = on_head * raw[c, g, p, t] + on_tail * raw[c, g, p, tiles + t]
         combine(X, 0, c, g)
 
     def solve_block(axis, minus):
@@ -362,16 +410,16 @@
 
         def walk(first, sign, count, visit, state):
             def block(g, state):
-                line = first + sign * unroll * g
+                line = first + sign * deep * g
                 row, coef_row = (line + 1) * PITCH, line * pitch + axis * tiles
 
                 def one(u, state):
                     at = lambda array, t: array[pl.ds(coef_row + t + u * (sign * pitch), 1), :]
                     return visit(pl.ds(row + u * (sign * PITCH), SUB), at, state)
 
-                return lax.fori_loop(0, min(count, unroll), one, state, unroll=True)
-
-            return lax.fori_loop(0, max(count // unroll, 1), block, state)
+                return lax.fori_loop(0, min(count, deep), one, state, unroll=True)
+
+            return lax.fori_loop(0, max(count // deep, 1), block, state)
 
         def eliminate(mult):
             def visit(here, at, state):
@@ -417,8 +465,8 @@
             return visit
 
         for first, sign, visit, state in ((lo, -1, substitute(m2, cn), low_s), (hi, 1, substitute(d2, an), high_s)):
-            state = walk(first + sign, sign, unroll - 1, visit, tuple(state))
-            walk(first + sign * unroll, sign, half - unroll, visit, state)
+            state = walk(first + sign, sign, deep - 1, visit, tuple(state))
+            walk(first + sign * deep, sign, half - deep, visit, state)
 
     def each_unit(body, count=units):
         lax.fori_loop(0, count, lambda u, carry: (body(u // parts_of, lax.rem(u, parts_of)), carry)[1], 0)
@@ -430,6 +478,11 @@
         def unit(g, carry):
             turn(qs, rs, c, Y, X, g * UNIT, UNIT, every, ends_of(X, 0, c, g), correct=False, explicit=True)
             publish_raw(c, g)
+
+            @pl.when((c == 0) & (g == 0))
+            def _():
+                spread_y()
+
             return carry
 
         await_halo(c)
@@ -445,14 +498,15 @@
 
     each_chunk(start_x)
     solve_block(X, True)
+    reduce_lines(Y)
+    await_raw(0, 0, raw.shape[3])
     reduce_lines(X)
-    reduce_lines(Y)
-    sent = gc_x.at[pl.ds(0, parts_x - 1)]
-    pltpu.make_async_copy(sent, sent, load_sem).wait()
-    sent = gc_y.at[pl.ds(0, parts_y - 1)]
-    pltpu.make_async_copy(sent, sent, load_sem).wait()
 
     def first_to_y(c, g):
+        @pl.when((c > 0) | (g > 0))
+        def _():
+            await_raw(c, g, 2 * tiles)
+
         neighbours_raw(c, g)
         turn(qs, rs, c, X, Y, g * UNIT, UNIT, every, ends_of(Y, 0, c, g))
         publish(Y, 0, c, g)
@@ -473,38 +527,43 @@
         neighbours(Y, STEPS - 1, c, g)
         turn(qs, out, c, Y, X, g * UNIT, UNIT, every, scale=0.5, step_out=SUB)
 
-    each_unit(finish, units - 1)
-    neighbours(Y, STEPS - 1, chunks - 1, parts_of - 1)
+    each_unit(finish, units - parts_of)
+    for g in range(parts_of):
+        neighbours(Y, STEPS - 1, chunks - 1, g, g)
 
 
 def finish_kernel(done, qs, w2, v2, ss, out, fresh, sem):
-    chunks, tiles = done.shape[:2]
-    lines, pitch, last = done.shape[2] // SUB, 2 * tiles, chunks - 1
-    base = SUB - UNIT
-
-    def place(c, t, src):
-        return pltpu.make_async_copy(src.reshape(lines, SUB, LANES), out.at[:, pl.ds(c * SUB, SUB), pl.ds(t * LANES, LANES)],
-                                     sem.at[c * tiles + t])
-
-    copies = [place(c, t, done.at[c, t]) for c in range(last) for t in range(tiles)]
-    for copy in copies:
-        copy.start()
+    last, tiles, lines = done.shape[0] - 1, done.shape[1], done.shape[2] // SUB
+    pitch = 2 * tiles
+
+    def place(c, t, src, whole=False):
+        step = lines if whole else LANES
+        for first in range(0, lines, step):
+            copy = pltpu.make_async_copy(src.at[pl.ds(first * SUB, step * SUB)].reshape(step, SUB, LANES),
+                                         out.at[pl.ds(first, step), pl.ds(c * SUB, SUB), pl.ds(t * LANES, LANES)], sem.at[c * tiles + t])
+            if whole:
+                copy.wait()
+            else:
+                copy.start()
+
+    for c in range(last):
+        for t in range(tiles):
+            place(c, t, done.at[c, t])
     for kt in range(tiles):
-        fresh[kt] = done[last, kt]
-
         def column(f, carry):
             for lt in range(tiles):
                 rows = pl.ds(kt * LANES * pitch + tiles + lt, LANES, stride=pitch)
-                block = qs[last, lt, pl.ds((kt * LANES + 1) * PITCH + base + f, LANES, stride=PITCH), :]
-                block = block + w2[rows, :] * ss[0, lt, pl.ds(f, 1), :] + v2[rows, :] * ss[1, lt, pl.ds(f, 1), :]
-                fresh[kt, pl.ds(lt * LANES * SUB + base + f, LANES, stride=SUB), :] = (block * 0.5).T
+                block = qs[last, lt, pl.ds((kt * LANES + 1) * PITCH + f, LANES, stride=PITCH), :]
+                near, far = (ss[f // UNIT, side, lt, pl.ds(f % UNIT, 1), :] for side in range(2))
+                block = block + w2[rows, :] * near + v2[rows, :] * far
+                fresh[kt, pl.ds(lt * LANES * SUB + f, LANES, stride=SUB), :] = (block * 0.5).T
             return carry
 
-        lax.fori_loop(0, UNIT, column, 0, unroll=True)
-        copies.append(place(last, kt, fresh.at[kt]))
-        copies[-1].start()
-    for copy in copies:
-        copy.wait()
+        lax.fori_loop(0, SUB, column, 0, unroll=True)
+        place(last, kt, fresh.at[kt])
+    for c in range(last + 1):
+        for t in range(tiles):
+            place(c, t, done.at[c, t] if c < last else fresh.at[t], whole=True)
 
 
 def solution(mesh):
@@ -530,17 +589,17 @@
         message = (4 * tiles, LANES)
         scratch = [
             pltpu.VMEM((6, n, n), F32), big, big, *([packed] * 15),
-            pltpu.VMEM((2,) + message, F32), pltpu.VMEM((parts_x,) + message, F32), pltpu.VMEM((parts_y,) + message, F32),
+            pltpu.VMEM(message, F32), pltpu.VMEM((parts_y,) + message, F32),
             table(parts_x), table(parts_y), sends, sends, line(parts_x), line(parts_y),
-            pltpu.VMEM((chunks, parts_of, parts_x, 2, tiles, UNIT, LANES), F32), pltpu.VMEM((chunks, parts_of, tiles, UNIT, LANES), F32),
-            small, small, dma, dma((2, chunks, parts_of)), dma((2, chunks, parts_of)), dma((2, chunks, parts_of)), dma((2,)),
+            pltpu.VMEM((chunks, parts_of, parts_x, 2 * tiles + 4 * tiles // UNIT, UNIT, LANES), F32), pltpu.VMEM((chunks, parts_of, tiles, UNIT, LANES), F32),
+            small, small, dma, dma, dma((2, chunks, parts_of)), dma((2, chunks, parts_of)), dma((2, chunks, parts_of)), dma,
         ]
         in_hbm = pl.BlockSpec(memory_space=pltpu.HBM)
         turned = jnp.transpose(field, (0, 2, 1))
         in_vmem = pl.BlockSpec(memory_space=pltpu.VMEM)
         shape = lambda *dims: jax.ShapeDtypeStruct(dims, F32)
         handed = (shape(chunks, tiles, n * SUB, LANES), shape(chunks, tiles, plane, LANES), shape(n * 2 * tiles, LANES),
-                  shape(n * 2 * tiles, LANES), shape(2, tiles, UNIT, LANES))
+                  shape(n * 2 * tiles, LANES), shape(parts_of, 2, tiles, UNIT, LANES))
         handed = pl.pallas_call(
             functools.partial(adi_kernel, (("row", parts_x), ("col", parts_y)), strides),
             out_shape=handed, in_specs=[in_hbm] * 7, out_specs=(in_vmem,) * len(handed), scratch_shapes=scratch,

time: 37.3 us -> 37.2 us (level)
  no operation moved by 1% of the time
where the time goes in v6:
time: 37.2 us; the launch traced here: 37.1 us
  Pallas kernels  37.1 us (100%)
    pallas_call x1, Pallas kernels, local_steps(): pl.pallas_call(functools.partial(adi_kernel, (('row', parts_x), ('col', p...  35 us
    pallas_call x1, Pallas kernels, local_steps(): pl.pallas_call(finish_kernel, out_shape=jax.ShapeDtypeStruct(turned.shape...  2.06 us

profile of v6, /device:TPU:97, one launch (start us, length us, event | category | flops | bytes accessed | tf_op | source)
XLA Modules:
  0.0 37.1 jit_solution(13288267606068683934)
XLA Ops:
  0.0 35.0 %adi_steps.1 = (f32[2,2,2048,128]{3,2,1,0:T(8,128)S(1)}, f32[2,2,2344,128]{3,2,1,0:T(8,128)S(1)}, f32[1024,128]{1,0:T(8,128)S(1)}, f32[1024,128]{1,0:T(8,128)S(1)}, f32[2,2,2,4,128]{4,3,2,1,0:T(4,128)S(1)}) custom-call(f32[256,16,256]{2,1,0:T(8,128)} %bitcast.2, f32[256,256]{1,0:T(8,128)} %lower_x.1, f32[256,256]{1,0:T(8,128)} %diag_x.1, ...), custom_call_target="tpu_custom_call" | custom-call | tf_op jit(solution)/shard_map/adi_steps/pallas_call | solution.py:603
  35.0 2.1 %finish.1 = f32[256,16,256]{2,1,0:T(8,128)} custom-call(f32[2,2,2048,128]{3,2,1,0:T(8,128)S(1)} %get-tuple-element.10.done, f32[2,2,2344,128]{3,2,1,0:T(8,128)S(1)} %get-tuple-element.11.qs, f32[1024,128]{1,0:T(8,128)S(1)} %get-tuple-element.12.w2, f32[1024,128]{1,0:T(8,128)S(1)} %get-tuple-element.13.v2, f32[2,2,2,4,128]{4,3,2,1,0:T(4,128)S(1)} %get-tuple-element.14.ss), custom_call_target="tpu_custom_call" | custom-call | tf_op jit(solution)/shard_map/finish/pallas_call | solution.py:609

commit v7 on v6

--- a/solution.py
+++ b/solution.py
@@ -46,8 +46,9 @@
         return [lax.rem(pos[axis] + off, count) for off in offs]
 
     def field_piece(c, t, first=0, count=n):
+        late = c == chunks - 1 and t == tiles - 1 and first > 0
         return pltpu.make_async_copy(field.at[pl.ds(first, count), pl.ds(c * SUB, SUB), pl.ds(t * LANES, LANES)],
-                                     out.at[c, t, pl.ds(first * SUB, count * SUB)].reshape(count, SUB, LANES), send_sem.at[t, c, 0])
+                                     out.at[c, t, pl.ds(first * SUB, count * SUB)].reshape(count, SUB, LANES), recv_x.at[1, 0, 0] if late else send_sem.at[t, c, 0])
 
     def load_field(c):
         for t in range(tiles):
@@ -80,13 +81,13 @@
     def each_chunk(body):
         lax.fori_loop(0, chunks, lambda c, carry: (body(c), carry)[1], 0)
 
-    def turn(src, dst, c, axis, to, base, many, lts, ends=None, step_in=PITCH, step_out=PITCH, correct=True, explicit=False, scale=None,
+    def turn(src, dst, c, axis, to, base, many, lts, ends=None, kts=None, step_in=PITCH, step_out=PITCH, correct=True, explicit=False, scale=None,
              g_ss=0):
         group = 2
 
         def column(g, carry):
             fs = [g * group + u for u in range(group)]
-            for kt in every:
+            for kt in kts or every:
                 heads, tails = [None] * group, [None] * group
                 for lt in lts:
                     rows = pl.ds(kt * (LANES * pitch) + (axis * tiles + lt), LANES, stride=pitch)
@@ -105,7 +106,7 @@
                             block = own * block - (low * src[c, lt, pl.ds(origin - step_in, LANES, stride=step_in), :]
                                                    + high * src[c, lt, pl.ds(origin + step_in, LANES, stride=step_in), :])
                         if correct:
-                            block = block + near * ss[g_ss, 0, lt, pl.ds(f, 1), :] + far * ss[g_ss, 1, lt, pl.ds(f, 1), :]
+                            block = block + near * ss[g_ss, 0, pl.ds(lt * UNIT + f, 1), :] + far * ss[g_ss, 1, pl.ds(lt * UNIT + f, 1), :]
                         if scale is not None:
                             block = block * scale
                         flipped = block.T
@@ -117,8 +118,8 @@
                             tails[u] = s if tails[u] is None else tails[u] + s
                 if ends:
                     for u, f in enumerate(fs):
-                        ends[0][kt, pl.ds(f, 1), :] = jnp.sum(heads[u], axis=0, keepdims=True)
-                        ends[1][kt, pl.ds(f, 1), :] = jnp.sum(tails[u], axis=0, keepdims=True)
+                        ends[0][pl.ds(kt * UNIT + f, 1), :] = jnp.sum(heads[u], axis=0, keepdims=True)
+                        ends[1][pl.ds(kt * UNIT + f, 1), :] = jnp.sum(tails[u], axis=0, keepdims=True)
             return carry
 
         lax.fori_loop(0, many // group, column, 0, unroll=True)
@@ -172,8 +173,13 @@
         if c == chunks - 1:
             pack_x()
         for t in range(tiles):
-            field_piece(c, t).wait()
-            turn(out, qs, c, X, Y, 0, SUB, (t,), step_in=SUB, correct=False)
+            if c < chunks - 1 or t < tiles - 1:
+                field_piece(c, t).wait()
+                turn(out, qs, c, X, Y, 0, SUB, (t,), step_in=SUB, correct=False)
+            else:
+                for kt in every:
+                    field_piece(c, t, kt * LANES, LANES).wait()
+                    turn(out, qs, c, X, Y, 0, SUB, (t,), kts=(kt,), step_in=SUB, correct=False)
         if c == 0:
             pl.semaphore_wait(barrier, parts_x + parts_y - 2)
         send_halo(c)
@@ -219,11 +225,10 @@
                 dp, dq, ep, eq = dp * scale_d, dq * scale_d, ep * scale_e, eq * scale_e
         return dp, dq, c_prev, ep, eq, a_next
 
-    lax.fori_loop(0, n // long, pivots, (one, zero, zero, one, zero, zero))
 
     low_half = lax.broadcasted_iota(jnp.int32, (SUB, LANES), 0) < pitch
     blocks = n * pitch // SUB
-    step_rows = 8
+    step_rows = long * pitch // SUB
 
     def ratios(g, state):
         prev_m, next_d = state
@@ -245,7 +250,10 @@
             next_d = turned
         return prev_m, next_d
 
-    lax.fori_loop(0, blocks // step_rows, ratios, (blank, blank))
+    stretches = n // long
+    state = lax.fori_loop(1, stretches, lambda g, state: (lambda later: (pivots(g, state[0]), later))(ratios(g - 1, state[1])),
+                          (pivots(0, (one, zero, zero, one, zero, zero)), (blank, blank)))
+    ratios(stretches - 1, state[1])
 
     first, last = pl.ds(0, pitch), pl.ds((n - 1) * pitch, pitch)
 
@@ -274,8 +282,7 @@
             yield q * tiles, -0.5 * ref[pl.ds(line * pitch + axis * tiles, tiles), :]
 
     for row, values in block_ends(X):
-        for t in every:
-            raw[0, 0, pos[X], 2 * tiles + (row + t) // UNIT, pl.ds((row + t) % UNIT, 1), :] = values[t:t + 1]
+        raw[0, 0, pos[X], 2, pl.ds(row, tiles), :] = values
 
     def spread_y():
         for row, values in block_ends(Y):
@@ -294,7 +301,7 @@
             pltpu.make_async_copy(arrived, arrived, load_sem).wait()
             part = lambda p, q: gc[p, pl.ds(q * tiles, tiles), :]
         else:
-            part = lambda p, q: raw[0, 0, p, 2 * tiles + q * tiles // UNIT, pl.ds(q * tiles % UNIT, tiles), :]
+            part = lambda p, q: raw[0, 0, p, 2, pl.ds(q * tiles, tiles), :]
         nil = jnp.zeros((tiles, LANES), F32)
         unit = jnp.ones((tiles, LANES), F32)
         mu, rho, tau = [None] * count, [None] * count, [None] * count
@@ -326,7 +333,11 @@
             onward = -omega[p - 1] * high[p - 1] if p else nil
             high[p] = jnp.where(me + 1 == p, unit, jnp.where(p > me + 1, onward, nil))
         table = reduced[axis]
-        put = lambda index, value: table.__setitem__((pl.ds(index * tiles, tiles), slice(None)), value)
+
+        def put(index, value):
+            for t in every:
+                table[index, pl.ds(t * UNIT, UNIT), :] = jnp.broadcast_to(value[t:t + 1], (UNIT, LANES))
+
         for p in range(count):
             put(p, k11 * low[p] + k12 * high[p] + jnp.where(me == p, -k11 * tau_b, nil))
             put(count + 1 + p, k21 * low[p] + k22 * high[p] + jnp.where(me == p, -k21 * tau_b, nil))
@@ -341,12 +352,9 @@
 
     def publish(axis, stage, c, g):
         count, table, way = parts[axis], reduced[axis], lax.rem(stage, 2)
-        for t in every:
-            head, tail = exch[axis][way, c, g, pos[axis], t], gt[c, g, t]
-            mu = table[pl.ds((2 * count + 2) * tiles + t, 1), :]
-            nu = table[pl.ds((2 * count + 3) * tiles + t, 1), :]
-            send[axis][c, g, 1, t] = tail + mu * head
-            send[axis][c, g, 0, t] = head + nu * tail
+        head, tail = exch[axis][way, c, g, pos[axis]], gt[c, g]
+        send[axis][c, g, 1] = tail + table[2 * count + 2] * head
+        send[axis][c, g, 0] = head + table[2 * count + 3] * tail
         for other in others(axis):
             sel = jnp.where(other > pos[axis], 1, 0)
             pltpu.make_async_remote_copy(
@@ -356,13 +364,12 @@
 
     def combine(axis, way, c, g, g_ss=0):
         count, table = parts[axis], reduced[axis]
-        for t in every:
-            for side in range(2):
-                base = side * (count + 1) * tiles + t
-                total = table[pl.ds(base + count * tiles, 1), :] * gt[c, g, t]
-                for p in range(count):
-                    total = total + table[pl.ds(base + p * tiles, 1), :] * exch[axis][way, c, g, p, t]
-                ss[g_ss, side, t] = total
+        for side in range(2):
+            base = side * (count + 1)
+            terms = [table[base + count] * gt[c, g]] + [table[base + p] * exch[axis][way, c, g, p] for p in range(count)]
+            while len(terms) > 1:
+                terms = [a + b for a, b in zip(terms[::2], terms[1::2])] + terms[len(terms) // 2 * 2:]
+            ss[g_ss, side] = terms[0]
 
     def neighbours(axis, stage, c, g, g_ss=0):
         way = lax.rem(stage, 2)
@@ -372,9 +379,8 @@
         combine(axis, way, c, g, g_ss)
 
     def publish_raw(c, g):
-        for t in every:
-            raw[c, g, pos[X], t] = exch[X][0, c, g, pos[X], t]
-            raw[c, g, pos[X], tiles + t] = gt[c, g, t]
+        raw[c, g, pos[X], 0] = exch[X][0, c, g, pos[X]]
+        raw[c, g, pos[X], 1] = gt[c, g]
 
         def send_raw(c, g, some):
             for other in others(X):
@@ -388,7 +394,7 @@
 
         @pl.when((c > 0) | (g > 0))
         def _():
-            send_raw(c, g, pl.ds(0, 2 * tiles))
+            send_raw(c, g, pl.ds(0, 2))
 
     def await_raw(c, g, blocks):
         arrived = raw.at[c, g, pl.ds(0, parts_x - 1), pl.ds(0, blocks)]
@@ -397,11 +403,8 @@
 
     def neighbours_raw(c, g):
         count = parts_x
-        for t in every:
-            for p in range(count):
-                on_head = red_x[pl.ds((2 * count + 4 + p) * tiles + t, 1), :]
-                on_tail = red_x[pl.ds((3 * count + 4 + p) * tiles + t, 1), :]
-                exch[X][0, c, g, p, t] = on_head * raw[c, g, p, t] + on_tail * raw[c, g, p, tiles + t]
+        for p in range(count):
+            exch[X][0, c, g, p] = (red_x[2 * count + 4 + p] * raw[c, g, p, 0] + red_x[3 * count + 4 + p] * raw[c, g, p, 1])
         combine(X, 0, c, g)
 
     def solve_block(axis, minus):
@@ -505,7 +508,7 @@
     def first_to_y(c, g):
         @pl.when((c > 0) | (g > 0))
         def _():
-            await_raw(c, g, 2 * tiles)
+            await_raw(c, g, 2)
 
         neighbours_raw(c, g)
         turn(qs, rs, c, X, Y, g * UNIT, UNIT, every, ends_of(Y, 0, c, g))
@@ -554,7 +557,7 @@
             for lt in range(tiles):
                 rows = pl.ds(kt * LANES * pitch + tiles + lt, LANES, stride=pitch)
                 block = qs[last, lt, pl.ds((kt * LANES + 1) * PITCH + f, LANES, stride=PITCH), :]
-                near, far = (ss[f // UNIT, side, lt, pl.ds(f % UNIT, 1), :] for side in range(2))
+                near, far = (ss[f // UNIT, side, pl.ds(lt * UNIT + f % UNIT, 1), :] for side in range(2))
                 block = block + w2[rows, :] * near + v2[rows, :] * far
                 fresh[kt, pl.ds(lt * LANES * SUB + f, LANES, stride=SUB), :] = (block * 0.5).T
             return carry
@@ -582,16 +585,16 @@
         big = pltpu.VMEM((chunks, tiles, plane, LANES), F32)
         dma = pltpu.SemaphoreType.DMA
         parts_of = SUB // UNIT
-        sends = pltpu.VMEM((chunks, parts_of, 2, tiles, UNIT, LANES), F32)
-        line = lambda count: pltpu.VMEM((2, chunks, parts_of, count, tiles, UNIT, LANES), F32)
-        table = lambda count: pltpu.VMEM(((4 * count + 4) * tiles, LANES), F32)
+        sends = pltpu.VMEM((chunks, parts_of, 2, tiles * UNIT, LANES), F32)
+        line = lambda count: pltpu.VMEM((2, chunks, parts_of, count, tiles * UNIT, LANES), F32)
+        table = lambda count: pltpu.VMEM((4 * count + 4, tiles * UNIT, LANES), F32)
         small = pltpu.VMEM((2, chunks, tiles, SUB, LANES), F32)
         message = (4 * tiles, LANES)
         scratch = [
             pltpu.VMEM((6, n, n), F32), big, big, *([packed] * 15),
             pltpu.VMEM(message, F32), pltpu.VMEM((parts_y,) + message, F32),
             table(parts_x), table(parts_y), sends, sends, line(parts_x), line(parts_y),
-            pltpu.VMEM((chunks, parts_of, parts_x, 2 * tiles + 4 * tiles // UNIT, UNIT, LANES), F32), pltpu.VMEM((chunks, parts_of, tiles, UNIT, LANES), F32),
+            pltpu.VMEM((chunks, parts_of, parts_x, 3, tiles * UNIT, LANES), F32), pltpu.VMEM((chunks, parts_of, tiles * UNIT, LANES), F32),
             small, small, dma, dma, dma((2, chunks, parts_of)), dma((2, chunks, parts_of)), dma((2, chunks, parts_of)), dma,
         ]
         in_hbm = pl.BlockSpec(memory_space=pltpu.HBM)
@@ -599,7 +602,7 @@
         in_vmem = pl.BlockSpec(memory_space=pltpu.VMEM)
         shape = lambda *dims: jax.ShapeDtypeStruct(dims, F32)
         handed = (shape(chunks, tiles, n * SUB, LANES), shape(chunks, tiles, plane, LANES), shape(n * 2 * tiles, LANES),
-                  shape(n * 2 * tiles, LANES), shape(parts_of, 2, tiles, UNIT, LANES))
+                  shape(n * 2 * tiles, LANES), shape(parts_of, 2, tiles * UNIT, LANES))
         handed = pl.pallas_call(
             functools.partial(adi_kernel, (("row", parts_x), ("col", parts_y)), strides),
             out_shape=handed, in_specs=[in_hbm] * 7, out_specs=(in_vmem,) * len(handed), scratch_shapes=scratch,

time: 37.2 us -> 37 us (level)
  no operation moved by 1% of the time
where the time goes in v7:
time: 37 us; the launch traced here: 36.9 us
  Pallas kernels  36.9 us (100%)
    pallas_call x1, Pallas kernels, local_steps(): pl.pallas_call(functools.partial(adi_kernel, (('row', parts_x), ('col', p...  34.8 us
    pallas_call x1, Pallas kernels, local_steps(): pl.pallas_call(finish_kernel, out_shape=jax.ShapeDtypeStruct(turned.shape...  2.06 us

profile of v7, /device:TPU:97, one launch (start us, length us, event | category | flops | bytes accessed | tf_op | source)
XLA Modules:
  0.0 36.9 jit_solution(7434491565870132004)
XLA Ops:
  0.0 34.8 %adi_steps.1 = (f32[2,2,2048,128]{3,2,1,0:T(8,128)S(1)}, f32[2,2,2344,128]{3,2,1,0:T(8,128)S(1)}, f32[1024,128]{1,0:T(8,128)S(1)}, f32[1024,128]{1,0:T(8,128)S(1)}, f32[2,2,8,128]{3,2,1,0:T(8,128)S(1)}) custom-call(f32[256,16,256]{2,1,0:T(8,128)} %bitcast.2, f32[256,256]{1,0:T(8,128)} %lower_x.1, f32[256,256]{1,0:T(8,128)} %diag_x.1, f32[256,256]{1,0:T(8,128)} %upper_x.1, ...), custom_call_target="tpu_custom_call" | custom-call | tf_op jit(solution)/shard_map/adi_steps/pallas_call | solution.py:606
  34.8 2.1 %finish.1 = f32[256,16,256]{2,1,0:T(8,128)} custom-call(f32[2,2,2048,128]{3,2,1,0:T(8,128)S(1)} %get-tuple-element.10.done, f32[2,2,2344,128]{3,2,1,0:T(8,128)S(1)} %get-tuple-element.11.qs, f32[1024,128]{1,0:T(8,128)S(1)} %get-tuple-element.12.w2, f32[1024,128]{1,0:T(8,128)S(1)} %get-tuple-element.13.v2, f32[2,2,8,128]{3,2,1,0:T(8,128)S(1)} %get-tuple-element.14.ss), custom_call_target="tpu_custom_call" | custom-call | tf_op jit(solution)/shard_map/finish/pallas_call | solution.py:612
